TPU v7x, 512 devices: a whole 4x8x8 slice. The times are simulated.
512 devices in a mesh: gx: 16 (over y_hi, z), gy: 4 (over y_lo), gz: 8 (over x, core).
Axes of the slice: x: 4, y: 8 (y_hi: 2, y_lo: 4; y = y_hi * 4 + y_lo), z: 8, core: 2. Of those that a mesh axis runs over, the one named last changes fastest.
Arguments:
- pair: bfloat16 [512, 512, 128], P('gx', ('gy', 'gz')), may hold values from -6 to 6
- pair_mask: int32 [512, 512], P('gx', ('gy', 'gz')), may hold values 0 or 1
- in_gain: float32 [128], replicated, may hold values from 0.1 to 1.9
- in_bias: float32 [128], replicated, may hold values from -3 to 3
- proj_weight: bfloat16 [128, 512], replicated, may hold values from -0.5 to 0.5
- gate_weight: bfloat16 [128, 128], replicated, may hold values from -0.5 to 0.5
- out_gain: float32 [128], replicated, may hold values from 0.1 to 1.9
- out_bias: float32 [128], replicated, may hold values from -3 to 3
- out_weight: bfloat16 [128, 128], replicated, may hold values from -0.5 to 0.5
Outputs:
- update: bfloat16 [512, 512, 128], P('gx', ('gy', 'gz'))
All inputs are finite; a program needn't handle non-finite values. No bound on the sum of `pair_mask` on one device may be relied on, other than what follows from the above.
Results may differ from a plain program's by a relative error of at most 0.0071.
Values may be sent and summed in bfloat16 or wider, within the bound.
No kernel may reach another device: no remote copies, remote signals or barrier semaphores. Data moves between devices by JAX's collectives and lax.ppermute only.
A program may use at most 64 MiB of HBM per device.

v0:
```python
import jax
import jax.numpy as jnp
from jax import lax
from jax.sharding import Mesh
from jax.sharding import PartitionSpec as P

GX = ("gx_0", "gx_1")


def sent_to_all(x, axis):
    copies = jnp.broadcast_to(x, (lax.axis_size(axis), *x.shape))
    return lax.all_to_all(copies, axis, split_axis=0, concat_axis=0, tiled=True)


def in_order(tiles, dim):
    tiles = jnp.moveaxis(tiles, 0, dim)
    dims = tiles.shape
    return tiles.reshape(*dims[:dim], dims[dim] * dims[dim + 1], *dims[dim + 2 :])


def gathered_copies(x, axis, dim):
    tiles = sent_to_all(x, axis)
    return in_order(tiles, dim)


def in_one_piece(arrays, axis, dim, along):
    both = jnp.concatenate(arrays, axis=along)
    result, at, gathered = (gathered_copies(both, axis, dim), 0, [])
    for a in arrays:
        gathered.append(lax.slice_in_dim(result, at, at + a.shape[along], axis=along))
        at += a.shape[along]
    return tuple(gathered)


def stacked_from(x, axes, sequence):
    tiles = x
    for k in sequence:
        tiles = lax.all_gather(tiles, axes[k])
    done = sequence[::-1]
    back = [done.index(k) for k in range(len(axes))]
    tiles = tiles.transpose(*back, *range(len(axes), tiles.ndim))
    return tiles.reshape(-1, *x.shape)


def gathered_by_axis(x, axes, sequence, dim):
    return in_order(stacked_from(x, axes, sequence), dim)


def in_blocks(x, dim, size):
    before, after = (x.shape[:dim], x.shape[dim + 1 :])
    return jnp.moveaxis(x.reshape(*before, size, -1, *after), dim, 0)


def sent_and_summed(x, axis, dim):
    size = lax.axis_size(axis)
    tiles = lax.all_to_all(in_blocks(x, dim, size), axis, 0, 0, tiled=True)
    return jnp.sum(tiles.astype(jnp.float32), axis=0)


def normalize(values, gain, bias):
    average = jnp.mean(values, axis=-1, keepdims=True)
    centered = values - average
    variance = jnp.mean(centered * centered, axis=-1, keepdims=True)
    return centered * lax.rsqrt(variance + 1e-05) * gain + bias


def project(tile, mask_value, in_gain, in_bias, proj_weight):
    hidden = proj_weight.shape[1] // 4
    normed = normalize(tile.astype(jnp.float32), in_gain, in_bias).astype(jnp.bfloat16)
    projected = jnp.einsum("rwc,cd->rwd", normed, proj_weight, preferred_element_type=jnp.float32)
    left_side = (
        jax.nn.sigmoid(projected[:, :, :hidden]) * projected[:, :, hidden : 2 * hidden] * mask_value
    ).astype(jnp.bfloat16)
    right_side = (
        jax.nn.sigmoid(projected[:, :, 2 * hidden : 3 * hidden])
        * projected[:, :, 3 * hidden :]
        * mask_value
    ).astype(jnp.bfloat16)
    return (normed, left_side, right_side)


def on_device(
    pair, pair_mask, in_gain, in_bias, proj_weight, gate_weight, out_gain, out_bias, out_weight
):
    mask_value = pair_mask.astype(jnp.float32)[:, :, None]
    normed, left_side, own_right = project(pair, mask_value, in_gain, in_bias, proj_weight)
    left_slab, right_slab = in_one_piece((left_side, own_right), "gy", 1, 0)
    every_row = gathered_by_axis(own_right, GX, (0, 1), 0)
    row_panel = lax.all_to_all(every_row, "gy", split_axis=0, concat_axis=1, tiled=True)
    summed = sent_and_summed(
        jnp.einsum("jkc,ikc->jic", row_panel, left_slab, preferred_element_type=jnp.float32).astype(
            jnp.bfloat16
        ),
        "gz",
        0,
    )
    triangle = jnp.transpose(summed, (1, 0, 2))
    tri_normed = normalize(triangle, out_gain, out_bias).astype(jnp.bfloat16)
    gating = jax.nn.sigmoid(
        jnp.einsum("rwc,cd->rwd", normed, gate_weight, preferred_element_type=jnp.float32)
    )
    mixed = jnp.einsum("rwh,hc->rwc", tri_normed, out_weight, preferred_element_type=jnp.float32)
    return (gating * mixed).astype(jnp.bfloat16)


def solution(mesh):
    finer = Mesh(
        mesh.devices.reshape(2, 8, mesh.shape["gy"], mesh.shape["gz"]), ("gx_0", "gx_1", "gy", "gz")
    )
    in_specs = (P(GX, ("gy", "gz"), None), P(GX, ("gy", "gz")), P(), P(), P(), P(), P(), P(), P())
    out_specs = P(GX, ("gy", "gz"), None)
    return jax.shard_map(
        on_device, mesh=finer, in_specs=in_specs, out_specs=out_specs, check_vma=False
    )
```

profile of v0, /device:TPU:1, one launch (start us, length us, event | category | flops | bytes accessed | tf_op | source)
XLA Modules:
  0.0 162.5 jit_solution(5244915075156663408)
XLA Ops:
  6.5 0.0 copy-start
  6.5 0.0 all-gather.4.cloned.1.call-start
  6.5 0.7 convert_element_type.32
  7.3 0.1 copy.54
  7.4 1.0 convert_reduce_fusion.1
  8.4 0.1 copy.50
  8.5 0.1 copy.51
  8.6 1.1 fusion.7
  9.7 0.1 copy.52
  9.8 0.1 copy.53
  9.9 0.0 copy-done
  9.9 1.3 fusion.21
  11.2 0.2 fusion.17
  11.3 11.9 %all-gather = bf16[64,16,128]{2,1,0:T(8,128)(2,1)} all-gather(bf16[32,16,128]{2,1,0:T(8,128)(2,1)S(1)} %get-tuple-element.6), channel_id=2, replica_groups=mesh['gx_0'=2,'gx_1'=8,'gy'=4,'gz'=8] {'gx_0'}, dimensions={0}, use_global_device_ids=true | all-gather | bytes 393216 | tf_op jit(solution)/shard_map/all_gather | solution.py:38
  23.3 0.0 all-gather.4.cloned.1.call-update
  23.3 1.1 broadcast_in_dim.2
  24.4 3.9 %all-to-all-start = ((bf16[4,64,16,128]{3,2,1,0:T(8,128)(2,1)}), bf16[4,64,16,128]{3,2,1,0:T(8,128)(2,1)S(1)}, u32[]{:S(2)}, u32[]{:S(2)}) async-start(bf16[4,64,16,128]{3,2,1,0:T(8,128)(2,1)} %broadcast_in_dim.2), calls=%async_computation | async-start | bytes 2097152 | tf_op jit(solution)/shard_map/all_to_all | solution.py:12
  28.3 41.2 %all-gather.4.cloned.1.call-done = bf16[16,32,16,128]{3,2,1,0:T(8,128)(2,1)} async-done(((bf16[2,32,16,128]{3,2,1,0:T(8,128)(2,1)}), bf16[16,32,16,128]{3,2,1,0:T(8,128)(2,1)}) %all-gather.4.cloned.1.call-update) | async-done | bytes 2097168 | tf_op jit(solution)/shard_map/all_gather | solution.py:38
  69.5 3.4 %copy.56 = bf16[2,8,32,16,128]{4,3,2,1,0:T(8,128)(2,1)} copy(bf16[2,8,32,16,128]{4,3,2,0,1:T(8,128)(2,1)} %bitcast.38) | data formatting | bytes 4194304 | tf_op jit(solution)/shard_map/transpose | solution.py:41
  72.9 0.0 all-to-all-done
  72.9 4.3 %all-to-all-start.1 = ((bf16[512,16,128]{2,1,0:T(8,128)(2,1)}), bf16[512,16,128]{2,1,0:T(8,128)(2,1)S(1)}, u32[]{:S(2)}, u32[]{:S(2)}) async-start(bf16[512,16,128]{2,1,0:T(8,128)(2,1)} %bitcast.7), calls=%async_computation.1 | async-start | bytes 4194304 | tf_op jit(solution)/shard_map/all_to_all | solution.py:89
  77.2 0.3 copy.64
  77.5 0.8 slice.28
  78.4 2.5 %copy.58 = bf16[32,64,128]{1,0,2:T(8,128)(2,1)S(1)} copy(bf16[32,64,128]{2,1,0:T(8,128)(2,1)} %bitcast.37) | data formatting | bytes 1048576 | tf_op jit(solution)/shard_map/slice | solution.py:30
  80.8 44.1 %all-to-all-done.1 = bf16[512,16,128]{2,1,0:T(8,128)(2,1)S(1)} async-done(((bf16[512,16,128]{2,1,0:T(8,128)(2,1)}), bf16[512,16,128]{2,1,0:T(8,128)(2,1)S(1)}, u32[]{:S(2)}, u32[]{:S(2)}) %all-to-all-start.1) | async-done | bytes 2097184 | tf_op jit(solution)/shard_map/all_to_all | solution.py:89
  125.0 3.8 %copy.57 = bf16[128,4,16,128]{0,2,1,3:T(8,128)(2,1)} copy(bf16[128,4,16,128]{3,2,0,1:T(8,128)(2,1)S(1)} %bitcast.34) | data formatting | bytes 4194304 | tf_op jit(solution)/shard_map/all_to_all | solution.py:89
  128.8 2.2 %fusion = bf16[128,32,128]{0,1,2:T(8,128)(2,1)S(1)} fusion(bf16[32,64,128]{1,0,2:T(8,128)(2,1)S(1)} %copy.58, bf16[128,64,128]{0,1,2:T(8,128)(2,1)} %bitcast.35), kind=kOutput, calls=%fused_computation.2 | convolution fusion | flops 67633152 | bytes 3670016 | tf_op jit(solution)/shard_map/jkc,ikc->jic/dot_general | solution.py:91
  131.1 0.0 copy-start.1
  131.1 0.0 copy-start.3
  131.1 0.0 copy-start.4
  131.1 0.0 copy-start.7
  131.1 2.3 %copy.59 = bf16[128,32,128]{2,1,0:T(8,128)(2,1)} copy(bf16[128,32,128]{0,1,2:T(8,128)(2,1)S(1)} %fusion) | data formatting | bytes 2097152 | tf_op jit(solution)/shard_map/convert_element_type | solution.py:91
  133.4 5.6 %all-to-all-start.2 = ((bf16[8,16,32,128]{3,2,1,0:T(8,128)(2,1)}), bf16[8,16,32,128]{3,2,1,0:T(8,128)(2,1)S(1)}, u32[]{:S(2)}, u32[]{:S(2)}) async-start(bf16[8,16,32,128]{3,2,1,0:T(8,128)(2,1)} %bitcast.12), calls=%async_computation.2 | async-start | bytes 2097152 | tf_op jit(solution)/shard_map/all_to_all | solution.py:56
  139.0 0.0 copy-done.1
  139.0 0.0 copy-done.3
  139.1 0.0 copy-done.4
  139.1 0.0 copy-done.7
  139.1 0.0 copy-start.5
  139.1 0.0 copy-start.6
  139.1 0.0 copy-start.2
  139.1 0.3 fusion.3
  139.5 14.6 %all-to-all-done.2 = bf16[8,16,32,128]{3,2,1,0:T(8,128)(2,1)S(1)} async-done(((bf16[8,16,32,128]{3,2,1,0:T(8,128)(2,1)}), bf16[8,16,32,128]{3,2,1,0:T(8,128)(2,1)S(1)}, u32[]{:S(2)}, u32[]{:S(2)}) %all-to-all-start.2) | async-done | bytes 1048608 | tf_op jit(solution)/shard_map/all_to_all | solution.py:56
  154.0 0.1 convert_reduce_fusion
  154.2 0.1 bitcast_reduce_fusion
  154.3 0.3 multiply_reduce_fusion
  154.6 0.0 copy-done.5
  154.6 0.0 copy-done.6
  154.6 0.2 add_convert_fusion
  154.8 0.0 copy-done.2
  154.8 0.8 fusion.4
  (5 shorter events, 0.1 us)
Async XLA Ops:
  6.5 3.3 %copy-start = (bf16[128,512]{1,0:T(8,128)(2,1)S(1)}, bf16[128,512]{1,0:T(8,128)(2,1)}, u32[]{:S(2)}) copy-start(bf16[128,512]{1,0:T(8,128)(2,1)} %param.13) | copy-start | bytes 393220
  6.5 63.0 %all-gather.4.cloned.1.call-start = ((), (), s32[]{:S(2)}) async-start(), calls=%async_computation.3 | async-start | bytes 2359296 | tf_op jit(solution)/shard_map/all_gather | solution.py:38
  24.4 48.4 %all-to-all-start = ((bf16[4,64,16,128]{3,2,1,0:T(8,128)(2,1)}), bf16[4,64,16,128]{3,2,1,0:T(8,128)(2,1)S(1)}, u32[]{:S(2)}, u32[]{:S(2)}) async-start(bf16[4,64,16,128]{3,2,1,0:T(8,128)(2,1)} %broadcast_in_dim.2), calls=%async_computation | async-start | bytes 2097152 | tf_op jit(solution)/shard_map/all_to_all | solution.py:12
  72.9 52.1 %all-to-all-start.1 = ((bf16[512,16,128]{2,1,0:T(8,128)(2,1)}), bf16[512,16,128]{2,1,0:T(8,128)(2,1)S(1)}, u32[]{:S(2)}, u32[]{:S(2)}) async-start(bf16[512,16,128]{2,1,0:T(8,128)(2,1)} %bitcast.7), calls=%async_computation.1 | async-start | bytes 4194304 | tf_op jit(solution)/shard_map/all_to_all | solution.py:89
  131.1 8.0 %copy-start.1 = (bf16[32,16,128]{2,1,0:T(8,128)(2,1)S(1)}, bf16[32,16,128]{2,1,0:T(8,128)(2,1)}, u32[]{:S(2)}) copy-start(bf16[32,16,128]{2,1,0:T(8,128)(2,1)} %param.9) | copy-start | bytes 393220
  131.1 8.0 %copy-start.3 = (f32[128]{0:T(128)S(1)}, f32[128]{0:T(128)}, u32[]{:S(2)}) copy-start(f32[128]{0:T(128)} %param.12) | copy-start | bytes 1540
  131.1 8.0 %copy-start.4 = (f32[128]{0:T(128)S(1)}, f32[128]{0:T(128)}, u32[]{:S(2)}) copy-start(f32[128]{0:T(128)} %param.11) | copy-start | bytes 1540
  131.1 8.0 %copy-start.7 = (bf16[128,128]{1,0:T(8,128)(2,1)S(1)}, bf16[128,128]{1,0:T(8,128)(2,1)}, u32[]{:S(2)}) copy-start(bf16[128,128]{1,0:T(8,128)(2,1)} %param.14) | copy-start | bytes 98308
  133.4 20.6 %all-to-all-start.2 = ((bf16[8,16,32,128]{3,2,1,0:T(8,128)(2,1)}), bf16[8,16,32,128]{3,2,1,0:T(8,128)(2,1)S(1)}, u32[]{:S(2)}, u32[]{:S(2)}) async-start(bf16[8,16,32,128]{3,2,1,0:T(8,128)(2,1)} %bitcast.12), calls=%async_computation.2 | async-start | bytes 2097152 | tf_op jit(solution)/shard_map/all_to_all | solution.py:56
  139.1 15.5 %copy-start.5 = (f32[128]{0:T(128)S(1)}, f32[128]{0:T(128)}, u32[]{:S(2)}) copy-start(f32[128]{0:T(128)} %param.16) | copy-start | bytes 1540
  139.1 15.5 %copy-start.6 = (f32[128]{0:T(128)S(1)}, f32[128]{0:T(128)}, u32[]{:S(2)}) copy-start(f32[128]{0:T(128)} %param.15) | copy-start | bytes 1540
  139.1 15.7 %copy-start.2 = (bf16[128,128]{1,0:T(8,128)(2,1)S(1)}, bf16[128,128]{1,0:T(8,128)(2,1)}, u32[]{:S(2)}) copy-start(bf16[128,128]{1,0:T(8,128)(2,1)} %param.17) | copy-start | bytes 98308
Sparse Core Ops, SparseCore 0:
  23.4 46.0 all-gather.3
where the time goes:
time: 163 us
  waiting for transfers between devices  99.9 us (61%)
  local copies, waits for them, and re-layouts  14.6 us (9%)
  starting transfers between devices  13.9 us (9%)
  between operations  13.6 us (8%)
  blocking collectives  11.9 us (7%)
  matrix products  4.71 us (3%)
  other arithmetic  3.89 us (2%)
    all_to_all x1, waiting for transfers between devices, on_device(): lax.all_to_all(every_row, 'gy', split_axis=0, concat_axis=1, tiled=True)  44.1 us
    all_gather x1, waiting for transfers between devices, stacked_from(): tiles = lax.all_gather(tiles, axes[k])  41.2 us
    all_to_all x1, waiting for transfers between devices, sent_and_summed(): tiles = lax.all_to_all(in_blocks(x, dim, size), axis, 0, 0, tiled=True)  14.6 us
    all_gather x1, blocking collectives, stacked_from(): tiles = lax.all_gather(tiles, axes[k])  11.9 us
    all_to_all x1, starting transfers between devices, sent_and_summed(): tiles = lax.all_to_all(in_blocks(x, dim, size), axis, 0, 0, tiled=True)  5.65 us
    all_to_all x1, starting transfers between devices, on_device(): lax.all_to_all(every_row, 'gy', split_axis=0, concat_axis=1, tiled=True)  4.31 us
    all_to_all x1, starting transfers between devices, sent_to_all(): return lax.all_to_all(copies, axis, split_axis=0, concat_axis=0, tiled=True)  3.91 us
    all_to_all x1, local copies, waits for them, and re-layouts, on_device(): lax.all_to_all(every_row, 'gy', split_axis=0, concat_axis=1, tiled=True)  3.84 us
  transfers between devices with their start and end apart: 4, of which 3 were waited for; matrix products, arithmetic and copies ran while one was open for 5% of the time, Pallas kernels for 0%

commit v1 on v0

v1 whole, which is shorter than its diff:
```python
import functools

import jax
import jax.numpy as jnp
from jax import lax
from jax.experimental import pallas as pl
from jax.experimental.pallas import tpu as pltpu
from jax.sharding import Mesh
from jax.sharding import PartitionSpec as P

COLUMNS = ("co", "gy", "x")
OUT_ORDER = ("gx", *COLUMNS)
IN_ORDER = (*COLUMNS, "gx")
EPS = 1e-05
F32 = jnp.float32
BF16 = jnp.bfloat16


def lane_iota(shape):
    return lax.broadcasted_iota(jnp.int32, shape, len(shape) - 1)


def swap_bits(arrays, bits):
    arrays = list(arrays)
    lanes = lane_iota(arrays[0].shape)
    for pos, lane in bits:
        step, width = 1 << pos, 1 << lane
        high = (lanes & width) != 0
        for at in range(len(arrays)):
            if at & step:
                continue
            a, b = arrays[at], arrays[at + step]
            arrays[at] = jnp.where(high, pltpu.roll(b, width, 1), a)
            arrays[at + step] = jnp.where(high, b, pltpu.roll(a, 128 - width, 1))
    return arrays


def project_kernel(pair, mask, gain, bias, weight, sent, normed_out, rows):
    x = pair[...].astype(F32)
    centered = x - jnp.mean(x, axis=-1, keepdims=True)
    variance = jnp.mean(centered * centered, axis=-1, keepdims=True)
    normed = (centered * lax.rsqrt(variance + EPS) * gain[...] + bias[...]).astype(BF16)
    normed_out[...] = normed
    k_of_lane = lane_iota((16, 128)) & 15
    spread = (k_of_lane == lax.broadcasted_iota(jnp.int32, (16, 128), 0)).astype(BF16)
    masks = jnp.dot(mask[...].astype(F32).astype(BF16), spread, preferred_element_type=F32)
    own_row = (lane_iota((8, 128)) >> 4) == lax.broadcasted_iota(jnp.int32, (8, 128), 0)
    for q in range(4):
        projected = lax.dot_general(
            weight[...],
            normed[q * 128 : (q + 1) * 128],
            (((0,), (1,)), ((), ())),
            preferred_element_type=F32,
        )
        keep = jnp.sum(jnp.where(own_row, masks[q * 8 : (q + 1) * 8], 0.0), axis=0, keepdims=True)
        left = jax.nn.sigmoid(projected[:128]) * projected[128:256] * keep
        right = jax.nn.sigmoid(projected[256:384]) * projected[384:] * keep
        hi, lo = q // 2, q % 2
        for other in range(2):
            for c_hi in range(4):
                block = slice(c_hi * 32, (c_hi + 1) * 32)
                to_left = ((hi * 2 + other) * 4 + c_hi) * 4 + lo
                rows[pl.ds(to_left, 32, stride=64), :] = left[block]
                to_right = ((other * 2 + lo) * 4 + c_hi) * 4 + 2 + hi
                rows[pl.ds(to_right, 32, stride=64), :] = right[block]
    sent[...] = rows[...].astype(BF16)


def triangle_kernel(got, sent, rows, left, right, product):
    rows[...] = got[...].astype(F32)
    for slot in range(4):
        for g_hi in range(4):
            pieces = [
                rows[pl.ds((g_hi * 8 + g) * 64 + slot, 16, stride=4), :] for g in range(8)
            ]
            pieces = swap_bits(pieces, ((0, 4), (1, 5), (2, 6)))
            for r in range(8):
                piece = pieces[r].astype(BF16)
                lanes = pl.ds(g_hi * 128, 128)
                if slot < 2:
                    left[pl.ds(((r % 2 * 2 + slot) * 4 + r // 2) * 16, 16), lanes] = piece
                else:
                    right[pl.ds((r * 2 + slot - 2) * 16, 16), lanes] = piece
    product[...] = lax.dot_general(
        right[...], left[...], (((1,), (1,)), ((), ())), preferred_element_type=F32
    )
    for at in range(4):
        pieces = [
            product[pl.ds(v % 8 * 32 + at * 8, 8), pl.ds(v // 8 * 128, 128)] for v in range(16)
        ]
        pieces = swap_bits(pieces, ((0, 0), (1, 1), (2, 2), (3, 3)))
        for gx in range(16):
            sent[pl.ds(gx * 32 + at * 8, 8), :] = pieces[gx]


def mix_kernel(got, normed, gate_weight, gain, bias, out_weight, update):
    gating = jax.nn.sigmoid(jnp.dot(normed[...], gate_weight[...], preferred_element_type=F32))
    gains = jnp.broadcast_to(gain[...], (128, 128)).T
    biases = jnp.broadcast_to(bias[...], (128, 128)).T
    for ih in range(2):
        halves = []
        gates = gating[ih * 256 : (ih + 1) * 256].reshape(16, 2, 8, 128)
        for jh in range(2):
            triangle = got[pl.ds((ih * 2 + jh) * 128, 128), :]
            centered = triangle - jnp.mean(triangle, axis=0, keepdims=True)
            variance = jnp.mean(centered * centered, axis=0, keepdims=True)
            tri_normed = (centered * lax.rsqrt(variance + EPS) * gains + biases).astype(BF16)
            mixed = lax.dot_general(
                tri_normed, out_weight[...], (((0,), (0,)), ((), ())), preferred_element_type=F32
            )
            halves.append(mixed.reshape(16, 8, 128) * gates[:, jh])
        both = jnp.concatenate(halves, axis=1).reshape(256, 128)
        update[pl.ds(ih * 256, 256), :] = both.astype(BF16)


def local_call(kernel, outs, scratch=(), flops=1_000_000):
    vmem = pl.BlockSpec(memory_space=pltpu.VMEM)

    def call(*args):
        return pl.pallas_call(
            kernel,
            out_shape=outs,
            in_specs=[vmem] * len(args),
            out_specs=jax.tree.map(lambda _: vmem, outs),
            scratch_shapes=scratch,
            compiler_params=pltpu.CompilerParams(vmem_limit_bytes=16 << 20),
            cost_estimate=pl.CostEstimate(
                flops=flops, bytes_accessed=1 << 20, transcendentals=0
            ),
        )(*args)

    return call


def on_device(
    pair, pair_mask, in_gain, in_bias, proj_weight, gate_weight, out_gain, out_bias, out_weight
):
    shape = jax.ShapeDtypeStruct
    sent, normed = local_call(
        project_kernel,
        (shape((2048, 128), BF16), shape((512, 128), BF16)),
        [pltpu.VMEM((2048, 128), F32)],
    )(pair.reshape(512, 128), pair_mask, in_gain[None], in_bias[None], proj_weight)
    got = lax.all_to_all(sent.reshape(512, 4, 128), IN_ORDER, 0, 0, tiled=True)
    sums = local_call(
        triangle_kernel,
        shape((512, 128), F32),
        [
            pltpu.VMEM((2048, 128), F32),
            pltpu.VMEM((256, 512), BF16),
            pltpu.VMEM((256, 512), BF16),
            pltpu.VMEM((256, 256), F32),
        ],
    )(got.reshape(2048, 128))
    back = lax.all_to_all(sums.reshape(512, 1, 128), OUT_ORDER, 0, 0, tiled=True)
    update = local_call(mix_kernel, shape((512, 128), BF16))(
        back.reshape(512, 128), normed, gate_weight, out_gain[None], out_bias[None], out_weight
    )
    return update.reshape(32, 16, 128)


def solution(mesh):
    gx, gy, gz = (mesh.shape[name] for name in ("gx", "gy", "gz"))
    finer = Mesh(mesh.devices.reshape(gx, gy, gz // 2, 2), ("gx", "gy", "x", "co"))
    columns = ("gy", "x", "co")
    in_specs = (P("gx", columns, None), P("gx", columns), P(), P(), P(), P(), P(), P(), P())
    return jax.shard_map(
        on_device,
        mesh=finer,
        in_specs=in_specs,
        out_specs=P("gx", columns, None),
        check_vma=False,
    )
```

time: 163 us -> 80 us (0.49)
  waiting for transfers between devices: 99.9 us -> 0 us
  blocking collectives: 11.9 us -> 71 us
  starting transfers between devices: 13.9 us -> 0 us
  between operations: 13.6 us -> 0.04 us
  local copies, waits for them, and re-layouts: 14.6 us -> 3.92 us
  matrix products: 4.71 us -> 0 us
  Pallas kernels: 0 us -> 4.66 us
  other arithmetic: 3.89 us -> 0 us
    all_to_all x0 -> x2, blocking collectives: none -> 71 us  [the longest x1 44 us: on_device(): got = lax.all_to_all(sent.reshape(512, 4, 128), IN_ORDER, 0, 0, tiled=True)]
    all_to_all x3 -> x0, waiting for transfers between devices: 58.7 us -> none  [the longest x1 44.1 us: on_device(): lax.all_to_all(every_row, 'gy', split_axis=0, concat_axis=1, tiled=True)]
    all_gather x1 -> x0, waiting for transfers between devices: 41.2 us -> none  [stacked_from(): tiles = lax.all_gather(tiles, axes[k])]
    all_to_all x3 -> x0, starting transfers between devices: 13.9 us -> none  [the longest x1 5.65 us: sent_and_summed(): tiles = lax.all_to_all(in_blocks(x, dim, size), axis, 0, 0, tiled=True)]
    all_gather x1 -> x0, blocking collectives: 11.9 us -> none  [stacked_from(): tiles = lax.all_gather(tiles, axes[k])]
    dot_general x4 -> x0, matrix products: 4.71 us -> none  [the longest x1 2.25 us: on_device(): jnp.einsum('jkc,ikc->jic', row_panel, left_slab, preferred_element_type=j...]
    pallas_call x0 -> x3, Pallas kernels: none -> 4.66 us  [call(): pl.pallas_call(kernel, out_shape=outs, in_specs=[vmem] * len(args), out_s...]
    all_to_all x2 -> x0, local copies, waits for them, and re-layouts: 4.15 us -> none  [the longest x1 3.84 us: on_device(): lax.all_to_all(every_row, 'gy', split_axis=0, concat_axis=1, tiled=True)]
  transfers between devices with their start and end apart: 4 -> 0, of which waited for: 3 -> 0; matrix products, arithmetic and copies ran while one was open for 5% -> 0% of each run, Pallas kernels for 0% -> 0%
where the time goes in v1:
time: 80 us; the launch traced here: 79.7 us
  blocking collectives  71 us (89%)
  Pallas kernels  4.66 us (6%)
  local copies, waits for them, and re-layouts  3.92 us (5%)
    all_to_all x1, blocking collectives, on_device(): got = lax.all_to_all(sent.reshape(512, 4, 128), IN_ORDER, 0, 0, tiled=True)  44 us
    all_to_all x1, blocking collectives, on_device(): lax.all_to_all(sums.reshape(512, 1, 128), OUT_ORDER, 0, 0, tiled=True)  27.1 us
    pallas_call x3, Pallas kernels, call(): pl.pallas_call(kernel, out_shape=outs, in_specs=[vmem] * len(args), out_s...  4.66 us
    unnamed x17, local copies, waits for them, and re-layouts  3.92 us

profile of v1, /device:TPU:1, one launch (start us, length us, event | category | flops | bytes accessed | tf_op | source)
XLA Modules:
  0.0 79.7 jit_solution(6852958203178988318)
XLA Ops:
  0.0 0.8 copy.11.mask
  0.8 0.0 copy-start.4
  0.8 0.0 copy-start.5
  0.8 0.7 copy-done.4
  1.4 0.0 copy-done.5
  1.4 0.0 copy-start
  1.4 0.9 %copy-done = bf16[32,16,128]{2,1,0:T(8,128)(2,1)S(1)} copy-done((bf16[32,16,128]{2,1,0:T(8,128)(2,1)S(1)}, bf16[32,16,128]{2,1,0:T(8,128)(2,1)}, u32[]{:S(2)}) %copy-start) | copy-done | bytes 131096
  2.3 0.0 copy-start.1
  2.4 0.9 %copy-done.1 = bf16[128,512]{1,0:T(8,128)(2,1)S(1)} copy-done((bf16[128,512]{1,0:T(8,128)(2,1)S(1)}, bf16[128,512]{1,0:T(8,128)(2,1)}, u32[]{:S(2)}) %copy-start.1) | copy-done | bytes 131096
  3.3 1.4 %shard_map.91 = (bf16[2048,128]{1,0:T(8,128)(2,1)S(1)}, bf16[512,128]{1,0:T(8,128)(2,1)S(1)}) custom-call(bf16[512,128]{1,0:T(8,128)(2,1)S(1)} %bitcast.16, s32[32,16]{1,0:T(8,128)S(1)} %copy.11.mask, f32[1,128]{1,0:T(1,128)S(1)} %bitcast.17, f32[1,128]{1,0:T(1,128)S(1)} %bitcast.18, bf16[128,512]{1,0:T(8,128)(2,1)S(1)} %copy-done.1), custom_call_target="tpu_custom_call" | custom-call | flops 1000000 | bytes 1048576 | tf_op jit(solution)/shard_map/pallas_call | solution.py:120
  4.7 44.0 %all_to_all.10 = bf16[512,4,128]{2,1,0:T(4,128)(2,1)S(1)} all-to-all(bf16[512,4,128]{2,1,0:T(4,128)(2,1)S(1)} %bitcast.15), channel_id=1, replica_groups=mesh['gx'=16,'gy'=4,'x'=4,'co'=2] {'co','gy','x','gx'}, dimensions={0} | all-to-all | bytes 1048576 | tf_op jit(solution)/shard_map/all_to_all | solution.py:144
  48.6 2.3 %shard_map.92 = f32[512,128]{1,0:T(8,128)S(1)} custom-call(bf16[2048,128]{1,0:T(8,128)(2,1)S(1)} %bitcast.12), custom_call_target="tpu_custom_call" | custom-call | flops 1000000 | bytes 1048576 | tf_op jit(solution)/shard_map/pallas_call | solution.py:120
  50.9 0.0 copy-start.2
  50.9 0.0 copy-start.3
  50.9 27.1 %all_to_all.11 = f32[512,1,128]{2,1,0:T(1,128)S(1)} all-to-all(f32[512,1,128]{2,1,0:T(1,128)S(1)} %bitcast.13), channel_id=1, replica_groups=mesh['gx'=16,'gy'=4,'x'=4,'co'=2] {'gx','co','gy','x'}, dimensions={0} | all-to-all | bytes 524288 | tf_op jit(solution)/shard_map/all_to_all | solution.py:155
  78.0 0.0 copy-start.6
  78.0 0.0 copy-start.7
  78.0 0.0 copy-done.2
  78.0 0.0 copy-done.3
  78.0 0.6 copy-done.6
  78.6 0.0 copy-done.7
  78.7 1.0 %shard_map.93 = bf16[512,128]{1,0:T(8,128)(2,1)} custom-call(f32[512,128]{1,0:T(8,128)S(1)} %bitcast.14, bf16[512,128]{1,0:T(8,128)(2,1)S(1)} %get-tuple-element.8.normed, bf16[128,128]{1,0:T(8,128)(2,1)S(1)} %copy-done.2, f32[1,128]{1,0:T(1,128)S(1)} %bitcast.19, f32[1,128]{1,0:T(1,128)S(1)} %bitcast.20, bf16[128,128]{1,0:T(8,128)(2,1)S(1)} %copy-done.3), custom_call_target="tpu_custom_call" | custom-call | flops 1000000 | bytes 1048576 | tf_op jit(solution)/shard_map/pallas_call | solution.py:120
Async XLA Ops:
  0.8 0.7 copy-start.4
  0.8 0.7 copy-start.5
  1.4 0.9 %copy-start = (bf16[32,16,128]{2,1,0:T(8,128)(2,1)S(1)}, bf16[32,16,128]{2,1,0:T(8,128)(2,1)}, u32[]{:S(2)}) copy-start(bf16[32,16,128]{2,1,0:T(8,128)(2,1)} %param.9) | copy-start | bytes 393220
  2.3 0.9 %copy-start.1 = (bf16[128,512]{1,0:T(8,128)(2,1)S(1)}, bf16[128,512]{1,0:T(8,128)(2,1)}, u32[]{:S(2)}) copy-start(bf16[128,512]{1,0:T(8,128)(2,1)} %weight.1) | copy-start | bytes 393220
  50.9 27.1 %copy-start.2 = (bf16[128,128]{1,0:T(8,128)(2,1)S(1)}, bf16[128,128]{1,0:T(8,128)(2,1)}, u32[]{:S(2)}) copy-start(bf16[128,128]{1,0:T(8,128)(2,1)} %gate_weight.1) | copy-start | bytes 98308
  50.9 27.1 %copy-start.3 = (bf16[128,128]{1,0:T(8,128)(2,1)S(1)}, bf16[128,128]{1,0:T(8,128)(2,1)}, u32[]{:S(2)}) copy-start(bf16[128,128]{1,0:T(8,128)(2,1)} %out_weight.1) | copy-start | bytes 98308
  78.0 0.7 copy-start.6
  78.0 0.7 copy-start.7

commit v2 on v1

v2 whole, which is shorter than its diff:
```python
import jax
import jax.numpy as jnp
from jax import lax
from jax.experimental import pallas as pl
from jax.experimental.pallas import tpu as pltpu
from jax.sharding import Mesh
from jax.sharding import PartitionSpec as P

ROW_AXES = ("yh", "zh", "zl")
COLUMN_AXES = ("y1", "y0", "x1", "x0", "co")
IN_ORDER = (*COLUMN_AXES, "yh", "zl")
OUT_ORDER = ("zl", "yh", *COLUMN_AXES)
EPS = 1e-05
F32 = jnp.float32
BF16 = jnp.bfloat16


def lane_iota(shape):
    return lax.broadcasted_iota(jnp.int32, shape, len(shape) - 1)


def swap_bits(arrays, bits):
    arrays = list(arrays)
    lanes = lane_iota(arrays[0].shape)
    for pos, lane in bits:
        step, width = 1 << pos, 1 << lane
        high = (lanes & width) != 0
        for at in range(len(arrays)):
            if at & step:
                continue
            a, b = arrays[at], arrays[at + step]
            arrays[at] = jnp.where(high, pltpu.roll(b, width, 1), a)
            arrays[at + step] = jnp.where(high, b, pltpu.roll(a, 128 - width, 1))
    return arrays


def project_kernel(
    pair_hbm,
    mask_hbm,
    gain_hbm,
    bias_hbm,
    weight_hbm,
    out_gain_hbm,
    out_bias_hbm,
    sent,
    normed_out,
    scales,
    pair,
    mask,
    gain,
    bias,
    weight,
    rows,
    sems,
):
    copies = [
        pltpu.make_async_copy(source, target, sems.at[at])
        for at, (source, target) in enumerate(
            (
                (pair_hbm, pair),
                (weight_hbm, weight),
                (mask_hbm, mask),
                (gain_hbm, gain),
                (bias_hbm, bias),
                (out_gain_hbm, scales.at[pl.ds(0, 1)]),
                (out_bias_hbm, scales.at[pl.ds(1, 1)]),
            )
        )
    ]
    for copy in copies:
        copy.start()
    for copy in copies:
        copy.wait()
    x = pair[...].astype(F32)
    centered = x - jnp.mean(x, axis=-1, keepdims=True)
    variance = jnp.mean(centered * centered, axis=-1, keepdims=True)
    normed = (centered * lax.rsqrt(variance + EPS) * gain[...] + bias[...]).astype(BF16)
    normed_out[...] = normed
    k_of_lane = lane_iota((16, 128)) & 15
    spread = (k_of_lane == lax.broadcasted_iota(jnp.int32, (16, 128), 0)).astype(BF16)
    masks = lax.dot_general(
        mask[...].astype(F32).astype(BF16),
        spread,
        (((0,), (0,)), ((), ())),
        preferred_element_type=F32,
    )
    own_row = (lane_iota((8, 128)) >> 4) == lax.broadcasted_iota(jnp.int32, (8, 128), 0)
    for q in range(4):
        projected = lax.dot_general(
            weight[...],
            normed[q * 128 : (q + 1) * 128],
            (((0,), (1,)), ((), ())),
            preferred_element_type=F32,
        )
        keep = jnp.sum(jnp.where(own_row, masks[q * 8 : (q + 1) * 8], 0.0), axis=0, keepdims=True)
        left = jax.nn.sigmoid(projected[:128]) * projected[128:256] * keep
        right = jax.nn.sigmoid(projected[256:384]) * projected[384:] * keep
        for c_hi in range(4):
            block = slice(c_hi * 32, (c_hi + 1) * 32)
            at = (c_hi % 2 * 2 + c_hi // 2) * 8 + q * 2
            rows[pl.ds(at, 32, stride=32), :] = left[block]
            rows[pl.ds(at + 1, 32, stride=32), :] = right[block]
    sent[...] = rows[...].astype(BF16)


def sides_kernel(got, left, right, rows):
    rows[...] = got[...].astype(F32)
    for side, target in enumerate((left, right)):
        for g_hi in range(4):
            pieces = [
                rows[pl.ds((g_hi * 8 + g) * 32 + side, 16, stride=2), :] for g in range(8)
            ]
            pieces = swap_bits(pieces, ((0, 4), (1, 5), (2, 6)))
            for r in range(8):
                target[pl.ds(r * 16, 16), pl.ds(g_hi * 128, 128)] = pieces[r].astype(BF16)


def triangle_kernel(right, left, sent, product, rows):
    product[...] = lax.dot_general(
        right[...], left[...], (((1,), (1,)), ((), ())), preferred_element_type=F32
    )
    for zh in range(4):
        for yh_j in range(2):
            pieces = [product[pl.ds(zh * 128 + r * 16 + yh_j * 8, 8), :] for r in range(8)]
            pieces = swap_bits(pieces, ((0, 2), (1, 3)))
            for v in range(8):
                high, yh, zl = v >> 2, v >> 1 & 1, v & 1
                owner = zl * 64 + yh * 32 + yh_j * 16 + zh * 4
                rows[pl.ds(owner * 4 + high, 8, stride=2), :] = pieces[v]
    sent[...] = rows[...].astype(BF16)


def mix_kernel(got, normed, gate_weight, scales, out_weight, update, rows, mixed, ordered):
    rows[...] = got[...].astype(F32)
    gating = jax.nn.sigmoid(jnp.dot(normed[...], gate_weight[...], preferred_element_type=F32))
    gains = jnp.broadcast_to(scales[0:1, :], (128, 128)).T
    biases = jnp.broadcast_to(scales[1:2, :], (128, 128)).T
    for h in range(4):
        triangle = rows[pl.ds(h, 128, stride=4), :]
        centered = triangle - jnp.mean(triangle, axis=0, keepdims=True)
        variance = jnp.mean(centered * centered, axis=0, keepdims=True)
        tri_normed = (centered * lax.rsqrt(variance + EPS) * gains + biases).astype(BF16)
        mixed[pl.ds(h * 128, 128), :] = lax.dot_general(
            tri_normed, out_weight[...], (((0,), (0,)), ((), ())), preferred_element_type=F32
        )
        for s in range(4):
            for jj in range(4):
                ordered[pl.ds(s * 128 + h * 4 + jj, 8, stride=16), :] = mixed[
                    pl.ds(h * 128 + jj * 4 + s, 8, stride=16), :
                ]
    update[...] = (ordered[...] * gating).astype(BF16)


def local_call(kernel, outs, scratch=(), flops=1_000_000, space=pltpu.VMEM):
    vmem = pl.BlockSpec(memory_space=pltpu.VMEM)

    def call(*args):
        return pl.pallas_call(
            kernel,
            out_shape=outs,
            in_specs=[pl.BlockSpec(memory_space=space)] * len(args),
            out_specs=jax.tree.map(lambda _: vmem, outs),
            scratch_shapes=scratch,
            compiler_params=pltpu.CompilerParams(vmem_limit_bytes=16 << 20),
            cost_estimate=pl.CostEstimate(
                flops=flops, bytes_accessed=1 << 20, transcendentals=0
            ),
        )(*args)

    return call


def on_device(
    pair, pair_mask, in_gain, in_bias, proj_weight, gate_weight, out_gain, out_bias, out_weight
):
    shape = jax.ShapeDtypeStruct
    sent, normed, scales = local_call(
        project_kernel,
        (shape((1024, 128), BF16), shape((512, 128), BF16), shape((2, 128), F32)),
        [
            pltpu.VMEM((512, 128), BF16),
            pltpu.VMEM((16, 32), jnp.int32),
            pltpu.VMEM((1, 128), F32),
            pltpu.VMEM((1, 128), F32),
            pltpu.VMEM((128, 512), BF16),
            pltpu.VMEM((1024, 128), F32),
            pltpu.SemaphoreType.DMA((7,)),
        ],
        space=pltpu.HBM,
    )(
        pair.reshape(512, 128),
        pair_mask.T,
        in_gain[None],
        in_bias[None],
        proj_weight,
        out_gain[None],
        out_bias[None],
    )
    got = lax.all_to_all(sent.reshape(128, 8, 128), IN_ORDER, 0, 0, tiled=True)
    left, right = local_call(
        sides_kernel,
        (shape((128, 512), BF16), shape((128, 512), BF16)),
        [pltpu.VMEM((1024, 128), F32)],
    )(got.reshape(1024, 128))
    every_right = lax.all_gather(right, "zh", axis=0, tiled=True)
    sums = local_call(
        triangle_kernel,
        shape((512, 128), BF16),
        [pltpu.VMEM((512, 128), F32), pltpu.VMEM((512, 128), F32)],
    )(every_right, left)
    back = lax.all_to_all(sums.reshape(128, 4, 128), OUT_ORDER, 0, 0, tiled=True)
    update = local_call(
        mix_kernel,
        shape((512, 128), BF16),
        [pltpu.VMEM((512, 128), F32), pltpu.VMEM((512, 128), F32), pltpu.VMEM((512, 128), F32)],
    )(back.reshape(512, 128), normed, gate_weight, scales, out_weight)
    return update.reshape(32, 16, 128)


def solution(mesh):
    finer = Mesh(mesh.devices.reshape((2, 4) + (2,) * 6), ROW_AXES + COLUMN_AXES)
    in_specs = (
        P(ROW_AXES, COLUMN_AXES, None),
        P(ROW_AXES, COLUMN_AXES),
        P(),
        P(),
        P(),
        P(),
        P(),
        P(),
        P(),
    )
    return jax.shard_map(
        on_device,
        mesh=finer,
        in_specs=in_specs,
        out_specs=P(ROW_AXES, COLUMN_AXES, None),
        check_vma=False,
    )
```

time: 80 us -> 73.8 us (0.922)
  blocking collectives: 71 us -> 67.5 us
  local copies, waits for them, and re-layouts: 3.92 us -> 2.52 us
  Pallas kernels: 4.66 us -> 3.43 us
    all_to_all x2, blocking collectives: 71 us -> 47.3 us  [the longest x1 27.4 us: on_device(): got = lax.all_to_all(sent.reshape(128, 8, 128), IN_ORDER, 0, 0, tiled=True)]
    all_gather x0 -> x1, blocking collectives: none -> 20.2 us  [on_device(): every_right = lax.all_gather(right, 'zh', axis=0, tiled=True)]
    unnamed x17 -> x18, local copies, waits for them, and re-layouts: 3.92 us -> 2.52 us
    pallas_call x3 -> x4, Pallas kernels: 4.66 us -> 3.43 us  [call(): pl.pallas_call(kernel, out_shape=outs, in_specs=[pl.BlockSpec(memory_spac...]
where the time goes in v2:
time: 73.8 us; the launch traced here: 73.5 us
  blocking collectives  67.5 us (91%)
  Pallas kernels  3.43 us (5%)
  local copies, waits for them, and re-layouts  2.52 us (3%)
    all_to_all x1, blocking collectives, on_device(): got = lax.all_to_all(sent.reshape(128, 8, 128), IN_ORDER, 0, 0, tiled=True)  27.4 us
    all_gather x1, blocking collectives, on_device(): every_right = lax.all_gather(right, 'zh', axis=0, tiled=True)  20.2 us
    all_to_all x1, blocking collectives, on_device(): lax.all_to_all(sums.reshape(128, 4, 128), OUT_ORDER, 0, 0, tiled=True)  19.9 us
    pallas_call x4, Pallas kernels, call(): pl.pallas_call(kernel, out_shape=outs, in_specs=[pl.BlockSpec(memory_spac...  3.43 us
    unnamed x18, local copies, waits for them, and re-layouts  2.52 us

profile of v2, /device:TPU:1, one launch (start us, length us, event | category | flops | bytes accessed | tf_op | source)
XLA Modules:
  0.0 73.5 jit_solution(5141104900328431044)
XLA Ops:
  0.0 0.0 copy-start.4
  0.0 0.0 copy-start.8
  0.0 0.0 copy-start.5
  0.0 0.0 copy-start.6
  0.0 0.0 copy-start.7
  0.0 0.7 copy-done.4
  0.7 0.0 copy-done.8
  0.7 0.0 copy-done.5
  0.7 0.0 copy-done.6
  0.7 0.0 copy-done.7
  0.7 0.0 copy-start
  0.7 0.9 %copy-done = bf16[32,16,128]{2,1,0:T(8,128)(2,1)S(1)} copy-done((bf16[32,16,128]{2,1,0:T(8,128)(2,1)S(1)}, bf16[32,16,128]{2,1,0:T(8,128)(2,1)}, u32[]{:S(2)}) %copy-start) | copy-done | bytes 131096
  1.6 0.0 copy-start.1
  1.6 0.9 %copy-done.1 = bf16[128,512]{1,0:T(8,128)(2,1)S(1)} copy-done((bf16[128,512]{1,0:T(8,128)(2,1)S(1)}, bf16[128,512]{1,0:T(8,128)(2,1)}, u32[]{:S(2)}) %copy-start.1) | copy-done | bytes 131096
  2.5 1.3 %shard_map.91 = (bf16[1024,128]{1,0:T(8,128)(2,1)S(1)}, bf16[512,128]{1,0:T(8,128)(2,1)S(1)}, f32[2,128]{1,0:T(2,128)S(1)}) custom-call(bf16[512,128]{1,0:T(8,128)(2,1)S(1)} %bitcast.15, s32[16,32]{1,0:T(8,128)S(1)} %bitcast.16, f32[1,128]{1,0:T(1,128)S(1)} %bitcast.17, f32[1,128]{1,0:T(1,128)S(1)} %bitcast.18, bf16[128,512]{1,0:T(8,128)(2,1)S(1)} %copy-done.1, ...), custom_call_target="tpu_custom_call" | custom-call | flops 1000000 | bytes 1048576 | tf_op jit(solution)/shard_map/pallas_call | solution.py:158
  3.8 27.4 %all_to_all.10 = bf16[128,8,128]{2,1,0:T(8,128)(2,1)S(1)} all-to-all(bf16[128,8,128]{2,1,0:T(8,128)(2,1)S(1)} %bitcast.14), channel_id=1, replica_groups=mesh['yh'=2,'zh'=4,'zl'=2,'y1'=2,'y0'=2,'x1'=2,'x0'=2,'co'=2] {'y1','y0'..., dimensions={0} | all-to-all | bytes 524288 | tf_op jit(solution)/shard_map/all_to_all | solution.py:199
  31.3 0.5 shard_map.92
  31.8 20.2 %all_gather.3.right = bf16[512,512]{1,0:T(8,128)(2,1)S(1)} all-gather(bf16[128,512]{1,0:T(8,128)(2,1)S(1)} %get-tuple-element.11), channel_id=1, replica_groups=mesh['yh'=2,'zh'=4,'zl'=2,'y1'=2,'y0'=2,'x1'=2,'x0'=2,'co'=2] {'zh'}, dimensions={0}, use_global_device_ids=true | all-gather | bytes 655360 | tf_op jit(solution)/shard_map/all_gather | solution.py:205
  52.0 0.5 shard_map.93
  52.4 0.0 copy-start.2
  52.5 0.0 copy-start.3
  52.5 19.9 %all_to_all.11 = bf16[128,4,128]{2,1,0:T(4,128)(2,1)S(1)} all-to-all(bf16[128,4,128]{2,1,0:T(4,128)(2,1)S(1)} %bitcast.13), channel_id=1, replica_groups=mesh['yh'=2,'zh'=4,'zl'=2,'y1'=2,'y0'=2,'x1'=2,'x0'=2,'co'=2] {'zl','yh'..., dimensions={0} | all-to-all | bytes 262144 | tf_op jit(solution)/shard_map/all_to_all | solution.py:211
  72.3 0.0 copy-done.2
  72.3 0.0 copy-done.3
  72.3 1.1 %shard_map.94 = bf16[512,128]{1,0:T(8,128)(2,1)} custom-call(bf16[512,128]{1,0:T(8,128)(2,1)S(1)} %bitcast.12, bf16[512,128]{1,0:T(8,128)(2,1)S(1)} %get-tuple-element.13.normed, bf16[128,128]{1,0:T(8,128)(2,1)S(1)} %copy-done.2, f32[2,128]{1,0:T(2,128)S(1)} %get-tuple-element.14.scales, bf16[128,128]{1,0:T(8,128)(2,1)S(1)} %copy-done.3), custom_call_target="tpu_custom_call" | custom-call | flops 1000000 | bytes 1048576 | tf_op jit(solution)/shard_map/pallas_call | solution.py:158
Async XLA Ops:
  0.0 0.7 copy-start.4
  0.0 0.7 copy-start.8
  0.0 0.7 copy-start.5
  0.0 0.7 copy-start.6
  0.0 0.7 copy-start.7
  0.7 0.9 %copy-start = (bf16[32,16,128]{2,1,0:T(8,128)(2,1)S(1)}, bf16[32,16,128]{2,1,0:T(8,128)(2,1)}, u32[]{:S(2)}) copy-start(bf16[32,16,128]{2,1,0:T(8,128)(2,1)} %param.9) | copy-start | bytes 393220
  1.6 0.9 %copy-start.1 = (bf16[128,512]{1,0:T(8,128)(2,1)S(1)}, bf16[128,512]{1,0:T(8,128)(2,1)}, u32[]{:S(2)}) copy-start(bf16[128,512]{1,0:T(8,128)(2,1)} %weight_hbm.1) | copy-start | bytes 393220
  52.4 19.9 %copy-start.2 = (bf16[128,128]{1,0:T(8,128)(2,1)S(1)}, bf16[128,128]{1,0:T(8,128)(2,1)}, u32[]{:S(2)}) copy-start(bf16[128,128]{1,0:T(8,128)(2,1)} %gate_weight.1) | copy-start | bytes 98308
  52.5 19.9 %copy-start.3 = (bf16[128,128]{1,0:T(8,128)(2,1)S(1)}, bf16[128,128]{1,0:T(8,128)(2,1)}, u32[]{:S(2)}) copy-start(bf16[128,128]{1,0:T(8,128)(2,1)} %out_weight.1) | copy-start | bytes 98308

commit v3 on v2

--- a/solution.py
+++ b/solution.py
@@ -8,8 +8,7 @@
 
 ROW_AXES = ("yh", "zh", "zl")
 COLUMN_AXES = ("y1", "y0", "x1", "x0", "co")
-IN_ORDER = (*COLUMN_AXES, "yh", "zl")
-OUT_ORDER = ("zl", "yh", *COLUMN_AXES)
+ORDER = (*COLUMN_AXES, "yh", "zl")
 EPS = 1e-05
 F32 = jnp.float32
 BF16 = jnp.bfloat16
@@ -34,47 +33,19 @@
     return arrays
 
 
-def project_kernel(
-    pair_hbm,
-    mask_hbm,
-    gain_hbm,
-    bias_hbm,
-    weight_hbm,
-    out_gain_hbm,
-    out_bias_hbm,
-    sent,
-    normed_out,
-    scales,
-    pair,
-    mask,
-    gain,
-    bias,
-    weight,
-    rows,
-    sems,
-):
-    copies = [
-        pltpu.make_async_copy(source, target, sems.at[at])
-        for at, (source, target) in enumerate(
-            (
-                (pair_hbm, pair),
-                (weight_hbm, weight),
-                (mask_hbm, mask),
-                (gain_hbm, gain),
-                (bias_hbm, bias),
-                (out_gain_hbm, scales.at[pl.ds(0, 1)]),
-                (out_bias_hbm, scales.at[pl.ds(1, 1)]),
-            )
-        )
-    ]
-    for copy in copies:
-        copy.start()
-    for copy in copies:
-        copy.wait()
+def normalize_kernel(pair, normalized):
     x = pair[...].astype(F32)
     centered = x - jnp.mean(x, axis=-1, keepdims=True)
     variance = jnp.mean(centered * centered, axis=-1, keepdims=True)
-    normed = (centered * lax.rsqrt(variance + EPS) * gain[...] + bias[...]).astype(BF16)
+    normalized[...] = centered * lax.rsqrt(variance + EPS)
+
+
+def project_kernel(
+    normalized, mask, gain, bias, weight, out_gain, out_bias, sent, normed_out, scales, rows
+):
+    scales[0:1, :] = out_gain[...]
+    scales[1:2, :] = out_bias[...]
+    normed = (normalized[...] * gain[...] + bias[...]).astype(BF16)
     normed_out[...] = normed
     k_of_lane = lane_iota((16, 128)) & 15
     spread = (k_of_lane == lax.broadcasted_iota(jnp.int32, (16, 128), 0)).astype(BF16)
@@ -93,13 +64,12 @@
             preferred_element_type=F32,
         )
         keep = jnp.sum(jnp.where(own_row, masks[q * 8 : (q + 1) * 8], 0.0), axis=0, keepdims=True)
-        left = jax.nn.sigmoid(projected[:128]) * projected[128:256] * keep
-        right = jax.nn.sigmoid(projected[256:384]) * projected[384:] * keep
-        for c_hi in range(4):
-            block = slice(c_hi * 32, (c_hi + 1) * 32)
-            at = (c_hi % 2 * 2 + c_hi // 2) * 8 + q * 2
-            rows[pl.ds(at, 32, stride=32), :] = left[block]
-            rows[pl.ds(at + 1, 32, stride=32), :] = right[block]
+        rows[pl.ds(q * 2, 128, stride=8), :] = (
+            jax.nn.sigmoid(projected[:128]) * projected[128:256] * keep
+        )
+        rows[pl.ds(q * 2 + 1, 128, stride=8), :] = (
+            jax.nn.sigmoid(projected[256:384]) * projected[384:] * keep
+        )
     sent[...] = rows[...].astype(BF16)
 
 
@@ -120,13 +90,14 @@
         right[...], left[...], (((1,), (1,)), ((), ())), preferred_element_type=F32
     )
     for zh in range(4):
-        for yh_j in range(2):
-            pieces = [product[pl.ds(zh * 128 + r * 16 + yh_j * 8, 8), :] for r in range(8)]
+        for jh in range(2):
+            pieces = [product[pl.ds(zh * 128 + r * 16 + jh, 8, stride=2), :] for r in range(8)]
             pieces = swap_bits(pieces, ((0, 2), (1, 3)))
             for v in range(8):
-                high, yh, zl = v >> 2, v >> 1 & 1, v & 1
-                owner = zl * 64 + yh * 32 + yh_j * 16 + zh * 4
-                rows[pl.ds(owner * 4 + high, 8, stride=2), :] = pieces[v]
+                high, owner_row = v >> 2, v & 3
+                for yh in range(2):
+                    at = ((yh * 16 + zh * 4) * 4 + owner_row) * 4 + jh * 2 + high
+                    rows[pl.ds(at, 4, stride=16), :] = pieces[v][yh * 4 : yh * 4 + 4]
     sent[...] = rows[...].astype(BF16)
 
 
@@ -151,14 +122,14 @@
     update[...] = (ordered[...] * gating).astype(BF16)
 
 
-def local_call(kernel, outs, scratch=(), flops=1_000_000, space=pltpu.VMEM):
+def local_call(kernel, outs, scratch=(), flops=1_000_000):
     vmem = pl.BlockSpec(memory_space=pltpu.VMEM)
 
     def call(*args):
         return pl.pallas_call(
             kernel,
             out_shape=outs,
-            in_specs=[pl.BlockSpec(memory_space=space)] * len(args),
+            in_specs=[vmem] * len(args),
             out_specs=jax.tree.map(lambda _: vmem, outs),
             scratch_shapes=scratch,
             compiler_params=pltpu.CompilerParams(vmem_limit_bytes=16 << 20),
@@ -174,21 +145,13 @@
     pair, pair_mask, in_gain, in_bias, proj_weight, gate_weight, out_gain, out_bias, out_weight
 ):
     shape = jax.ShapeDtypeStruct
+    normalized = local_call(normalize_kernel, shape((512, 128), F32))(pair.reshape(512, 128))
     sent, normed, scales = local_call(
         project_kernel,
         (shape((1024, 128), BF16), shape((512, 128), BF16), shape((2, 128), F32)),
-        [
-            pltpu.VMEM((512, 128), BF16),
-            pltpu.VMEM((16, 32), jnp.int32),
-            pltpu.VMEM((1, 128), F32),
-            pltpu.VMEM((1, 128), F32),
-            pltpu.VMEM((128, 512), BF16),
-            pltpu.VMEM((1024, 128), F32),
-            pltpu.SemaphoreType.DMA((7,)),
-        ],
-        space=pltpu.HBM,
+        [pltpu.VMEM((1024, 128), F32)],
     )(
-        pair.reshape(512, 128),
+        normalized,
         pair_mask.T,
         in_gain[None],
         in_bias[None],
@@ -196,7 +159,7 @@
         out_gain[None],
         out_bias[None],
     )
-    got = lax.all_to_all(sent.reshape(128, 8, 128), IN_ORDER, 0, 0, tiled=True)
+    got = lax.all_to_all(sent.reshape(128, 8, 128), ORDER, 0, 0, tiled=True)
     left, right = local_call(
         sides_kernel,
         (shape((128, 512), BF16), shape((128, 512), BF16)),
@@ -208,7 +171,7 @@
         shape((512, 128), BF16),
         [pltpu.VMEM((512, 128), F32), pltpu.VMEM((512, 128), F32)],
     )(every_right, left)
-    back = lax.all_to_all(sums.reshape(128, 4, 128), OUT_ORDER, 0, 0, tiled=True)
+    back = lax.all_to_all(sums.reshape(128, 4, 128), ORDER, 0, 0, tiled=True)
     update = local_call(
         mix_kernel,
         shape((512, 128), BF16),

time: 73.8 us -> 70.9 us (0.961)
  blocking collectives: 67.5 us -> 66.2 us
  local copies, waits for them, and re-layouts: 2.52 us -> 1.62 us
    all_to_all x2, blocking collectives: 47.3 us -> 46 us  [the longest x1 27.4 us: on_device(): got = lax.all_to_all(sent.reshape(128, 8, 128), ORDER, 0, 0, tiled=True)]
    unnamed x18, local copies, waits for them, and re-layouts: 2.52 us -> 1.62 us
    pallas_call x4 -> x5, Pallas kernels: 3.43 us -> 2.79 us  [call(): pl.pallas_call(kernel, out_shape=outs, in_specs=[vmem] * len(args), out_s...]
where the time goes in v3:
time: 70.9 us; the launch traced here: 70.6 us
  blocking collectives  66.2 us (93%)
  Pallas kernels  2.79 us (4%)
  local copies, waits for them, and re-layouts  1.62 us (2%)
    all_to_all x1, blocking collectives, on_device(): got = lax.all_to_all(sent.reshape(128, 8, 128), ORDER, 0, 0, tiled=True)  27.4 us
    all_gather x1, blocking collectives, on_device(): every_right = lax.all_gather(right, 'zh', axis=0, tiled=True)  20.2 us
    all_to_all x1, blocking collectives, on_device(): back = lax.all_to_all(sums.reshape(128, 4, 128), ORDER, 0, 0, tiled=True)  18.6 us
    pallas_call x5, Pallas kernels, call(): pl.pallas_call(kernel, out_shape=outs, in_specs=[vmem] * len(args), out_s...  2.79 us
    unnamed x18, local copies, waits for them, and re-layouts  1.62 us

profile of v3, /device:TPU:1, one launch (start us, length us, event | category | flops | bytes accessed | tf_op | source)
XLA Modules:
  0.0 70.6 jit_solution(13436897394708504099)
XLA Ops:
  0.0 0.0 copy-start
  0.0 0.9 %copy-done = bf16[32,16,128]{2,1,0:T(8,128)(2,1)S(1)} copy-done((bf16[32,16,128]{2,1,0:T(8,128)(2,1)S(1)}, bf16[32,16,128]{2,1,0:T(8,128)(2,1)}, u32[]{:S(2)}) %copy-start) | copy-done | bytes 131096
  0.9 0.0 copy-start.1
  0.9 0.0 copy-start.7
  0.9 0.0 copy-start.8
  0.9 0.2 shard_map.91.normalized
  1.1 0.0 copy-start.4
  1.2 0.0 copy-start.5
  1.2 0.0 copy-start.6
  1.2 0.6 copy-done.1
  1.8 0.0 copy-done.7
  1.8 0.0 copy-done.8
  1.8 0.0 copy-done.4
  1.9 0.0 copy-done.5
  1.9 0.0 copy-done.6
  1.9 0.4 shard_map.92
  2.3 27.4 %all_to_all.10 = bf16[128,8,128]{2,1,0:T(8,128)(2,1)S(1)} all-to-all(bf16[128,8,128]{2,1,0:T(8,128)(2,1)S(1)} %bitcast.14), channel_id=1, replica_groups=mesh['yh'=2,'zh'=4,'zl'=2,'y1'=2,'y0'=2,'x1'=2,'x0'=2,'co'=2] {'y1','y0'..., dimensions={0} | all-to-all | bytes 524288 | tf_op jit(solution)/shard_map/all_to_all | solution.py:162
  29.7 0.5 shard_map.93
  30.2 20.2 %all_gather.3.right = bf16[512,512]{1,0:T(8,128)(2,1)S(1)} all-gather(bf16[128,512]{1,0:T(8,128)(2,1)S(1)} %get-tuple-element.11), channel_id=1, replica_groups=mesh['yh'=2,'zh'=4,'zl'=2,'y1'=2,'y0'=2,'x1'=2,'x0'=2,'co'=2] {'zh'}, dimensions={0}, use_global_device_ids=true | all-gather | bytes 655360 | tf_op jit(solution)/shard_map/all_gather | solution.py:168
  50.4 0.5 shard_map.94
  50.9 0.0 copy-start.2
  50.9 0.0 copy-start.3
  50.9 18.6 %all_to_all.11 = bf16[128,4,128]{2,1,0:T(4,128)(2,1)S(1)} all-to-all(bf16[128,4,128]{2,1,0:T(4,128)(2,1)S(1)} %bitcast.13), channel_id=1, replica_groups=mesh['yh'=2,'zh'=4,'zl'=2,'y1'=2,'y0'=2,'x1'=2,'x0'=2,'co'=2] {'y1','y0'..., dimensions={0} | all-to-all | bytes 262144 | tf_op jit(solution)/shard_map/all_to_all | solution.py:174
  69.5 0.0 copy-done.2
  69.5 0.0 copy-done.3
  69.5 1.1 %shard_map.95 = bf16[512,128]{1,0:T(8,128)(2,1)} custom-call(bf16[512,128]{1,0:T(8,128)(2,1)S(1)} %bitcast.12, bf16[512,128]{1,0:T(8,128)(2,1)S(1)} %get-tuple-element.13.normed, bf16[128,128]{1,0:T(8,128)(2,1)S(1)} %copy-done.2, f32[2,128]{1,0:T(2,128)S(1)} %get-tuple-element.14.scales, bf16[128,128]{1,0:T(8,128)(2,1)S(1)} %copy-done.3), custom_call_target="tpu_custom_call" | custom-call | flops 1000000 | bytes 1048576 | tf_op jit(solution)/shard_map/pallas_call | solution.py:129
Async XLA Ops:
  0.0 0.9 %copy-start = (bf16[32,16,128]{2,1,0:T(8,128)(2,1)S(1)}, bf16[32,16,128]{2,1,0:T(8,128)(2,1)}, u32[]{:S(2)}) copy-start(bf16[32,16,128]{2,1,0:T(8,128)(2,1)} %param.9) | copy-start | bytes 393220
  0.9 0.9 %copy-start.1 = (bf16[128,512]{1,0:T(8,128)(2,1)S(1)}, bf16[128,512]{1,0:T(8,128)(2,1)}, u32[]{:S(2)}) copy-start(bf16[128,512]{1,0:T(8,128)(2,1)} %weight.1) | copy-start | bytes 393220
  0.9 0.9 %copy-start.7 = (f32[128]{0:T(128)S(1)}, f32[128]{0:T(128)}, u32[]{:S(2)}) copy-start(f32[128]{0:T(128)} %param.15) | copy-start | bytes 1540
  0.9 0.9 %copy-start.8 = (f32[128]{0:T(128)S(1)}, f32[128]{0:T(128)}, u32[]{:S(2)}) copy-start(f32[128]{0:T(128)} %param.16) | copy-start | bytes 1540
  1.1 0.7 %copy-start.4 = (s32[32,16]{0,1:T(8,128)S(1)}, s32[32,16]{0,1:T(8,128)}, u32[]{:S(2)}) copy-start(s32[32,16]{0,1:T(8,128)} %param.10) | copy-start | bytes 6148
  1.2 0.7 copy-start.5
  1.2 0.7 copy-start.6
  50.9 18.6 %copy-start.2 = (bf16[128,128]{1,0:T(8,128)(2,1)S(1)}, bf16[128,128]{1,0:T(8,128)(2,1)}, u32[]{:S(2)}) copy-start(bf16[128,128]{1,0:T(8,128)(2,1)} %gate_weight.1) | copy-start | bytes 98308
  50.9 18.6 %copy-start.3 = (bf16[128,128]{1,0:T(8,128)(2,1)S(1)}, bf16[128,128]{1,0:T(8,128)(2,1)}, u32[]{:S(2)}) copy-start(bf16[128,128]{1,0:T(8,128)(2,1)} %out_weight.1) | copy-start | bytes 98308

commit v4 on v3

--- a/solution.py
+++ b/solution.py
@@ -33,19 +33,48 @@
     return arrays
 
 
-def normalize_kernel(pair, normalized):
+def project_kernel(
+    pair_hbm,
+    weight_hbm,
+    mask_hbm,
+    gain_hbm,
+    bias_hbm,
+    out_gain_hbm,
+    out_bias_hbm,
+    sent,
+    normed_out,
+    scales,
+    pair,
+    weight,
+    mask,
+    gain,
+    bias,
+    rows,
+    sems,
+):
+    moves = (
+        (pair_hbm, pair),
+        (gain_hbm, gain),
+        (bias_hbm, bias),
+        (weight_hbm, weight),
+        (mask_hbm, mask),
+        (out_gain_hbm, scales.at[pl.ds(0, 1)]),
+        (out_bias_hbm, scales.at[pl.ds(1, 1)]),
+    )
+    copies = [
+        pltpu.make_async_copy(source, target, sems.at[at])
+        for at, (source, target) in enumerate(moves)
+    ]
+    for copy in copies:
+        copy.start()
+    copies[0].wait()
     x = pair[...].astype(F32)
     centered = x - jnp.mean(x, axis=-1, keepdims=True)
     variance = jnp.mean(centered * centered, axis=-1, keepdims=True)
-    normalized[...] = centered * lax.rsqrt(variance + EPS)
-
-
-def project_kernel(
-    normalized, mask, gain, bias, weight, out_gain, out_bias, sent, normed_out, scales, rows
-):
-    scales[0:1, :] = out_gain[...]
-    scales[1:2, :] = out_bias[...]
-    normed = (normalized[...] * gain[...] + bias[...]).astype(BF16)
+    normalized = centered * lax.rsqrt(variance + EPS)
+    for copy in copies[1:]:
+        copy.wait()
+    normed = (normalized * gain[...] + bias[...]).astype(BF16)
     normed_out[...] = normed
     k_of_lane = lane_iota((16, 128)) & 15
     spread = (k_of_lane == lax.broadcasted_iota(jnp.int32, (16, 128), 0)).astype(BF16)
@@ -101,9 +130,10 @@
     sent[...] = rows[...].astype(BF16)
 
 
-def mix_kernel(got, normed, gate_weight, scales, out_weight, update, rows, mixed, ordered):
+def mix_kernel(
+    got, normed, gate_weight, scales, out_weight, update, rows, mixed, ordered, staged, sems
+):
     rows[...] = got[...].astype(F32)
-    gating = jax.nn.sigmoid(jnp.dot(normed[...], gate_weight[...], preferred_element_type=F32))
     gains = jnp.broadcast_to(scales[0:1, :], (128, 128)).T
     biases = jnp.broadcast_to(scales[1:2, :], (128, 128)).T
     for h in range(4):
@@ -114,27 +144,36 @@
         mixed[pl.ds(h * 128, 128), :] = lax.dot_general(
             tri_normed, out_weight[...], (((0,), (0,)), ((), ())), preferred_element_type=F32
         )
-        for s in range(4):
+    copies = []
+    for s in range(4):
+        block = pl.ds(s * 128, 128)
+        gating = jax.nn.sigmoid(
+            jnp.dot(normed[block, :], gate_weight[...], preferred_element_type=F32)
+        )
+        for h in range(4):
             for jj in range(4):
                 ordered[pl.ds(s * 128 + h * 4 + jj, 8, stride=16), :] = mixed[
                     pl.ds(h * 128 + jj * 4 + s, 8, stride=16), :
                 ]
-    update[...] = (ordered[...] * gating).astype(BF16)
-
-
-def local_call(kernel, outs, scratch=(), flops=1_000_000):
-    vmem = pl.BlockSpec(memory_space=pltpu.VMEM)
+        staged[block, :] = (ordered[block, :] * gating).astype(BF16)
+        copies.append(pltpu.make_async_copy(staged.at[block], update.at[block], sems.at[s]))
+        copies[s].start()
+    for copy in copies:
+        copy.wait()
+
+
+def local_call(kernel, outs, scratch=(), in_space=pltpu.VMEM, out_space=pltpu.VMEM):
 
     def call(*args):
         return pl.pallas_call(
             kernel,
             out_shape=outs,
-            in_specs=[vmem] * len(args),
-            out_specs=jax.tree.map(lambda _: vmem, outs),
+            in_specs=[pl.BlockSpec(memory_space=in_space)] * len(args),
+            out_specs=jax.tree.map(lambda _: pl.BlockSpec(memory_space=out_space), outs),
             scratch_shapes=scratch,
             compiler_params=pltpu.CompilerParams(vmem_limit_bytes=16 << 20),
             cost_estimate=pl.CostEstimate(
-                flops=flops, bytes_accessed=1 << 20, transcendentals=0
+                flops=1_000_000, bytes_accessed=1 << 20, transcendentals=0
             ),
         )(*args)
 
@@ -145,20 +184,29 @@
     pair, pair_mask, in_gain, in_bias, proj_weight, gate_weight, out_gain, out_bias, out_weight
 ):
     shape = jax.ShapeDtypeStruct
-    normalized = local_call(normalize_kernel, shape((512, 128), F32))(pair.reshape(512, 128))
+    inputs = (
+        pair.reshape(512, 128),
+        proj_weight,
+        pair_mask.T,
+        in_gain[None],
+        in_bias[None],
+        out_gain[None],
+        out_bias[None],
+    )
     sent, normed, scales = local_call(
         project_kernel,
         (shape((1024, 128), BF16), shape((512, 128), BF16), shape((2, 128), F32)),
-        [pltpu.VMEM((1024, 128), F32)],
-    )(
-        normalized,
-        pair_mask.T,
-        in_gain[None],
-        in_bias[None],
-        proj_weight,
-        out_gain[None],
-        out_bias[None],
-    )
+        [
+            pltpu.VMEM((512, 128), BF16),
+            pltpu.VMEM((128, 512), BF16),
+            pltpu.VMEM((16, 32), jnp.int32),
+            pltpu.VMEM((1, 128), F32),
+            pltpu.VMEM((1, 128), F32),
+            pltpu.VMEM((1024, 128), F32),
+            pltpu.SemaphoreType.DMA((7,)),
+        ],
+        in_space=pltpu.HBM,
+    )(*(pltpu.with_memory_space_constraint(a, pltpu.HBM) for a in inputs))
     got = lax.all_to_all(sent.reshape(128, 8, 128), ORDER, 0, 0, tiled=True)
     left, right = local_call(
         sides_kernel,
@@ -172,10 +220,12 @@
         [pltpu.VMEM((512, 128), F32), pltpu.VMEM((512, 128), F32)],
     )(every_right, left)
     back = lax.all_to_all(sums.reshape(128, 4, 128), ORDER, 0, 0, tiled=True)
+    block = pltpu.VMEM((512, 128), F32)
     update = local_call(
         mix_kernel,
         shape((512, 128), BF16),
-        [pltpu.VMEM((512, 128), F32), pltpu.VMEM((512, 128), F32), pltpu.VMEM((512, 128), F32)],
+        [block, block, block, pltpu.VMEM((512, 128), BF16), pltpu.SemaphoreType.DMA((4,))],
+        out_space=pltpu.HBM,
     )(back.reshape(512, 128), normed, gate_weight, scales, out_weight)
     return update.reshape(32, 16, 128)
 

time: 70.9 us -> 70.2 us (level)
  local copies, waits for them, and re-layouts: 1.62 us -> 0.01 us
  Pallas kernels: 2.79 us -> 3.76 us
    unnamed x18 -> x4, local copies, waits for them, and re-layouts: 1.62 us -> 0.01 us
    pallas_call x5 -> x4, Pallas kernels: 2.79 us -> 3.76 us  [call(): pl.pallas_call(kernel, out_shape=outs, in_specs=[pl.BlockSpec(memory_spac...]
where the time goes in v4:
time: 70.2 us; the launch traced here: 70 us
  blocking collectives  66.2 us (94%)
  Pallas kernels  3.76 us (5%)
    all_to_all x1, blocking collectives, on_device(): got = lax.all_to_all(sent.reshape(128, 8, 128), ORDER, 0, 0, tiled=True)  27.4 us
    all_gather x1, blocking collectives, on_device(): every_right = lax.all_gather(right, 'zh', axis=0, tiled=True)  20.2 us
    all_to_all x1, blocking collectives, on_device(): back = lax.all_to_all(sums.reshape(128, 4, 128), ORDER, 0, 0, tiled=True)  18.5 us
    pallas_call x4, Pallas kernels, call(): pl.pallas_call(kernel, out_shape=outs, in_specs=[pl.BlockSpec(memory_spac...  3.76 us

profile of v4, /device:TPU:1, one launch (start us, length us, event | category | flops | bytes accessed | tf_op | source)
XLA Modules:
  0.0 70.0 jit_solution(3309415001019553212)
XLA Ops:
  0.0 1.6 %shard_map.91 = (bf16[1024,128]{1,0:T(8,128)(2,1)S(1)}, bf16[512,128]{1,0:T(8,128)(2,1)S(1)}, f32[2,128]{1,0:T(2,128)S(1)}) custom-call(bf16[512,128]{1,0:T(8,128)(2,1)} %bitcast.15, bf16[128,512]{1,0:T(8,128)(2,1)} %weight_hbm.1, s32[16,32]{1,0:T(8,128)} %bitcast.16, f32[1,128]{1,0:T(1,128)} %bitcast.17, f32[1,128]{1,0:T(1,128)} %bitcast.18, ...), custom_call_target="tpu_custom_call" | custom-call | flops 1000000 | bytes 1048576 | tf_op jit(solution)/shard_map/pallas_call | solution.py:168
  1.6 27.4 %all_to_all.10 = bf16[128,8,128]{2,1,0:T(8,128)(2,1)S(1)} all-to-all(bf16[128,8,128]{2,1,0:T(8,128)(2,1)S(1)} %bitcast.14), channel_id=1, replica_groups=mesh['yh'=2,'zh'=4,'zl'=2,'y1'=2,'y0'=2,'x1'=2,'x0'=2,'co'=2] {'y1','y0'..., dimensions={0} | all-to-all | bytes 524288 | tf_op jit(solution)/shard_map/all_to_all | solution.py:210
  29.0 0.5 shard_map.92
  29.6 20.2 %all_gather.3.right = bf16[512,512]{1,0:T(8,128)(2,1)S(1)} all-gather(bf16[128,512]{1,0:T(8,128)(2,1)S(1)} %get-tuple-element.11), channel_id=1, replica_groups=mesh['yh'=2,'zh'=4,'zl'=2,'y1'=2,'y0'=2,'x1'=2,'x0'=2,'co'=2] {'zh'}, dimensions={0}, use_global_device_ids=true | all-gather | bytes 655360 | tf_op jit(solution)/shard_map/all_gather | solution.py:216
  49.7 0.5 shard_map.93
  50.2 0.0 copy-start
  50.3 0.0 copy-start.1
  50.3 18.5 %all_to_all.11 = bf16[128,4,128]{2,1,0:T(4,128)(2,1)S(1)} all-to-all(bf16[128,4,128]{2,1,0:T(4,128)(2,1)S(1)} %bitcast.13), channel_id=1, replica_groups=mesh['yh'=2,'zh'=4,'zl'=2,'y1'=2,'y0'=2,'x1'=2,'x0'=2,'co'=2] {'y1','y0'..., dimensions={0} | all-to-all | bytes 262144 | tf_op jit(solution)/shard_map/all_to_all | solution.py:222
  68.8 0.0 copy-done
  68.8 0.0 copy-done.1
  68.8 1.1 %shard_map.94 = bf16[512,128]{1,0:T(8,128)(2,1)} custom-call(bf16[512,128]{1,0:T(8,128)(2,1)S(1)} %bitcast.12, bf16[512,128]{1,0:T(8,128)(2,1)S(1)} %get-tuple-element.13.normed, bf16[128,128]{1,0:T(8,128)(2,1)S(1)} %copy-done, f32[2,128]{1,0:T(2,128)S(1)} %get-tuple-element.14.scales, bf16[128,128]{1,0:T(8,128)(2,1)S(1)} %copy-done.1), custom_call_target="tpu_custom_call" | custom-call | flops 1000000 | bytes 1048576 | tf_op jit(solution)/shard_map/pallas_call | solution.py:168
Async XLA Ops:
  50.2 18.6 %copy-start = (bf16[128,128]{1,0:T(8,128)(2,1)S(1)}, bf16[128,128]{1,0:T(8,128)(2,1)}, u32[]{:S(2)}) copy-start(bf16[128,128]{1,0:T(8,128)(2,1)} %gate_weight.1) | copy-start | bytes 98308
  50.3 18.6 %copy-start.1 = (bf16[128,128]{1,0:T(8,128)(2,1)S(1)}, bf16[128,128]{1,0:T(8,128)(2,1)}, u32[]{:S(2)}) copy-start(bf16[128,128]{1,0:T(8,128)(2,1)} %out_weight.1) | copy-start | bytes 98308

commit v5 on v4

--- a/solution.py
+++ b/solution.py
@@ -6,9 +6,9 @@
 from jax.sharding import Mesh
 from jax.sharding import PartitionSpec as P
 
-ROW_AXES = ("yh", "zh", "zl")
+ROW_AXES = ("yh", "z2", "z1", "z0")
 COLUMN_AXES = ("y1", "y0", "x1", "x0", "co")
-ORDER = (*COLUMN_AXES, "yh", "zl")
+ORDER = ("y1", "y0", "co", "z1", "z0", "yh", "z2")
 EPS = 1e-05
 F32 = jnp.float32
 BF16 = jnp.bfloat16
@@ -102,31 +102,31 @@
     sent[...] = rows[...].astype(BF16)
 
 
-def sides_kernel(got, left, right, rows):
+def partial_kernel(got, sent, left, right, rows):
     rows[...] = got[...].astype(F32)
     for side, target in enumerate((left, right)):
-        for g_hi in range(4):
-            pieces = [
-                rows[pl.ds((g_hi * 8 + g) * 32 + side, 16, stride=2), :] for g in range(8)
-            ]
+        for z in range(4):
+            pieces = [rows[pl.ds(g * 128 + z * 32 + side, 16, stride=2), :] for g in range(8)]
             pieces = swap_bits(pieces, ((0, 4), (1, 5), (2, 6)))
             for r in range(8):
-                target[pl.ds(r * 16, 16), pl.ds(g_hi * 128, 128)] = pieces[r].astype(BF16)
-
-
-def triangle_kernel(right, left, sent, product, rows):
-    product[...] = lax.dot_general(
-        right[...], left[...], (((1,), (1,)), ((), ())), preferred_element_type=F32
-    )
-    for zh in range(4):
+                target[pl.ds(z * 128 + r * 16, 16), :] = pieces[r].astype(BF16)
+    for z in range(4):
+        block = pl.ds(z * 128, 128)
+        sent[block, :] = lax.dot_general(
+            right[block, :], left[...], (((1,), (1,)), ((), ())), preferred_element_type=F32
+        ).astype(BF16)
+
+
+def sum_kernel(got, sent, total, rows):
+    for z in range(4):
+        lanes = pl.ds(z * 128, 128)
+        total[lanes, :] = sum(got[pl.ds(x * 128, 128), lanes].astype(F32) for x in range(4))
         for jh in range(2):
-            pieces = [product[pl.ds(zh * 128 + r * 16 + jh, 8, stride=2), :] for r in range(8)]
+            pieces = [total[pl.ds(z * 128 + r * 16 + jh, 8, stride=2), :] for r in range(8)]
             pieces = swap_bits(pieces, ((0, 2), (1, 3)))
             for v in range(8):
-                high, owner_row = v >> 2, v & 3
-                for yh in range(2):
-                    at = ((yh * 16 + zh * 4) * 4 + owner_row) * 4 + jh * 2 + high
-                    rows[pl.ds(at, 4, stride=16), :] = pieces[v][yh * 4 : yh * 4 + 4]
+                at = (z * 4 + (v & 3)) * 4 + jh * 2 + (v >> 2)
+                rows[pl.ds(at, 8, stride=64), :] = pieces[v]
     sent[...] = rows[...].astype(BF16)
 
 
@@ -208,17 +208,16 @@
         in_space=pltpu.HBM,
     )(*(pltpu.with_memory_space_constraint(a, pltpu.HBM) for a in inputs))
     got = lax.all_to_all(sent.reshape(128, 8, 128), ORDER, 0, 0, tiled=True)
-    left, right = local_call(
-        sides_kernel,
-        (shape((128, 512), BF16), shape((128, 512), BF16)),
-        [pltpu.VMEM((1024, 128), F32)],
+    side = pltpu.VMEM((512, 128), BF16)
+    partial = local_call(
+        partial_kernel, shape((512, 512), BF16), [side, side, pltpu.VMEM((1024, 128), F32)]
     )(got.reshape(1024, 128))
-    every_right = lax.all_gather(right, "zh", axis=0, tiled=True)
+    parts = lax.all_to_all(partial.reshape(4, 128, 512), ("x1", "x0"), 0, 0, tiled=True)
     sums = local_call(
-        triangle_kernel,
+        sum_kernel,
         shape((512, 128), BF16),
         [pltpu.VMEM((512, 128), F32), pltpu.VMEM((512, 128), F32)],
-    )(every_right, left)
+    )(parts.reshape(512, 512))
     back = lax.all_to_all(sums.reshape(128, 4, 128), ORDER, 0, 0, tiled=True)
     block = pltpu.VMEM((512, 128), F32)
     update = local_call(
@@ -231,7 +230,7 @@
 
 
 def solution(mesh):
-    finer = Mesh(mesh.devices.reshape((2, 4) + (2,) * 6), ROW_AXES + COLUMN_AXES)
+    finer = Mesh(mesh.devices.reshape((2,) * 9), ROW_AXES + COLUMN_AXES)
     in_specs = (
         P(ROW_AXES, COLUMN_AXES, None),
         P(ROW_AXES, COLUMN_AXES),

time: 70.2 us -> 68.7 us (0.979)
  blocking collectives: 66.2 us -> 64.6 us
    all_gather x1 -> x0, blocking collectives: 20.2 us -> none  [on_device(): every_right = lax.all_gather(right, 'zh', axis=0, tiled=True)]
    all_to_all x0 -> x1, blocking collectives: none -> 12.9 us  [on_device(): lax.all_to_all(partial.reshape(4, 128, 512), ('x1', 'x0'), 0, 0, tiled=True)]
    all_to_all x1, blocking collectives: 27.4 us -> 32.7 us  [on_device(): got = lax.all_to_all(sent.reshape(128, 8, 128), ORDER, 0, 0, tiled=True)]
where the time goes in v5:
time: 68.7 us; the launch traced here: 68.4 us
  blocking collectives  64.6 us (94%)
  Pallas kernels  3.77 us (5%)
    all_to_all x1, blocking collectives, on_device(): got = lax.all_to_all(sent.reshape(128, 8, 128), ORDER, 0, 0, tiled=True)  32.7 us
    all_to_all x1, blocking collectives, on_device(): back = lax.all_to_all(sums.reshape(128, 4, 128), ORDER, 0, 0, tiled=True)  19 us
    all_to_all x1, blocking collectives, on_device(): lax.all_to_all(partial.reshape(4, 128, 512), ('x1', 'x0'), 0, 0, tiled=True)  12.9 us
    pallas_call x4, Pallas kernels, call(): pl.pallas_call(kernel, out_shape=outs, in_specs=[pl.BlockSpec(memory_spac...  3.77 us

profile of v5, /device:TPU:1, one launch (start us, length us, event | category | flops | bytes accessed | tf_op | source)
XLA Modules:
  0.0 68.4 jit_solution(10852639418295379389)
XLA Ops:
  0.0 1.6 %shard_map.91 = (bf16[1024,128]{1,0:T(8,128)(2,1)S(1)}, bf16[512,128]{1,0:T(8,128)(2,1)S(1)}, f32[2,128]{1,0:T(2,128)S(1)}) custom-call(bf16[512,128]{1,0:T(8,128)(2,1)} %bitcast.19, bf16[128,512]{1,0:T(8,128)(2,1)} %weight_hbm.1, s32[16,32]{1,0:T(8,128)} %bitcast.20, f32[1,128]{1,0:T(1,128)} %bitcast.21, f32[1,128]{1,0:T(1,128)} %bitcast.22, ...), custom_call_target="tpu_custom_call" | custom-call | flops 1000000 | bytes 1048576 | tf_op jit(solution)/shard_map/pallas_call | solution.py:168
  1.6 32.7 %all_to_all.15 = bf16[128,8,128]{2,1,0:T(8,128)(2,1)S(1)} all-to-all(bf16[128,8,128]{2,1,0:T(8,128)(2,1)S(1)} %bitcast.18), channel_id=1, replica_groups=mesh['yh'=2,'z2'=2,'z1'=2,'z0'=2,'y1'=2,'y0'=2,'x1'=2,'x0'=2,'co'=2] {'y..., dimensions={0} | all-to-all | bytes 524288 | tf_op jit(solution)/shard_map/all_to_all | solution.py:210
  34.3 0.7 %shard_map.92 = bf16[512,512]{1,0:T(8,128)(2,1)S(1)} custom-call(bf16[1024,128]{1,0:T(8,128)(2,1)S(1)} %bitcast.15), custom_call_target="tpu_custom_call" | custom-call | flops 1000000 | bytes 1048576 | tf_op jit(solution)/shard_map/pallas_call | solution.py:168
  35.0 12.9 %all_to_all.16 = bf16[4,128,512]{2,1,0:T(8,128)(2,1)S(1)} all-to-all(bf16[4,128,512]{2,1,0:T(8,128)(2,1)S(1)} %bitcast.14), channel_id=1, replica_groups=mesh['yh'=2,'z2'=2,'z1'=2,'z0'=2,'y1'=2,'y0'=2,'x1'=2,'x0'=2,'co'=2] {'x..., dimensions={0} | all-to-all | bytes 1048576 | tf_op jit(solution)/shard_map/all_to_all | solution.py:215
  47.9 0.3 shard_map.93
  48.3 0.0 copy-start
  48.3 0.0 copy-start.1
  48.3 19.0 %all_to_all.17 = bf16[128,4,128]{2,1,0:T(4,128)(2,1)S(1)} all-to-all(bf16[128,4,128]{2,1,0:T(4,128)(2,1)S(1)} %bitcast.17), channel_id=1, replica_groups=mesh['yh'=2,'z2'=2,'z1'=2,'z0'=2,'y1'=2,'y0'=2,'x1'=2,'x0'=2,'co'=2] {'y..., dimensions={0} | all-to-all | bytes 262144 | tf_op jit(solution)/shard_map/all_to_all | solution.py:221
  67.3 0.0 copy-done
  67.3 0.0 copy-done.1
  67.3 1.1 %shard_map.94 = bf16[512,128]{1,0:T(8,128)(2,1)} custom-call(bf16[512,128]{1,0:T(8,128)(2,1)S(1)} %bitcast.16, bf16[512,128]{1,0:T(8,128)(2,1)S(1)} %get-tuple-element.9.normed, bf16[128,128]{1,0:T(8,128)(2,1)S(1)} %copy-done, f32[2,128]{1,0:T(2,128)S(1)} %get-tuple-element.10.scales, bf16[128,128]{1,0:T(8,128)(2,1)S(1)} %copy-done.1), custom_call_target="tpu_custom_call" | custom-call | flops 1000000 | bytes 1048576 | tf_op jit(solution)/shard_map/pallas_call | solution.py:168
Async XLA Ops:
  48.3 19.0 %copy-start = (bf16[128,128]{1,0:T(8,128)(2,1)S(1)}, bf16[128,128]{1,0:T(8,128)(2,1)}, u32[]{:S(2)}) copy-start(bf16[128,128]{1,0:T(8,128)(2,1)} %gate_weight.1) | copy-start | bytes 98308
  48.3 19.0 %copy-start.1 = (bf16[128,128]{1,0:T(8,128)(2,1)S(1)}, bf16[128,128]{1,0:T(8,128)(2,1)}, u32[]{:S(2)}) copy-start(bf16[128,128]{1,0:T(8,128)(2,1)} %out_weight.1) | copy-start | bytes 98308

commit v6 on v5

--- a/solution.py
+++ b/solution.py
@@ -52,11 +52,12 @@
     rows,
     sems,
 ):
+    quarters = [pl.ds(q * 128, 128) for q in range(4)]
     moves = (
-        (pair_hbm, pair),
+        *((pair_hbm.at[q], pair.at[q]) for q in quarters),
         (gain_hbm, gain),
         (bias_hbm, bias),
-        (weight_hbm, weight),
+        *((weight_hbm.at[:, q], weight.at[:, q]) for q in quarters),
         (mask_hbm, mask),
         (out_gain_hbm, scales.at[pl.ds(0, 1)]),
         (out_bias_hbm, scales.at[pl.ds(1, 1)]),
@@ -67,15 +68,18 @@
     ]
     for copy in copies:
         copy.start()
-    copies[0].wait()
-    x = pair[...].astype(F32)
-    centered = x - jnp.mean(x, axis=-1, keepdims=True)
-    variance = jnp.mean(centered * centered, axis=-1, keepdims=True)
-    normalized = centered * lax.rsqrt(variance + EPS)
-    for copy in copies[1:]:
+    normalized = []
+    for q in range(4):
+        copies[q].wait()
+        x = pair[quarters[q], :].astype(F32)
+        centered = x - jnp.mean(x, axis=-1, keepdims=True)
+        variance = jnp.mean(centered * centered, axis=-1, keepdims=True)
+        normalized.append(centered * lax.rsqrt(variance + EPS))
+    for copy in copies[4:]:
         copy.wait()
-    normed = (normalized * gain[...] + bias[...]).astype(BF16)
-    normed_out[...] = normed
+    normed = [(part * gain[...] + bias[...]).astype(BF16) for part in normalized]
+    for q in range(4):
+        normed_out[quarters[q], :] = normed[q]
     k_of_lane = lane_iota((16, 128)) & 15
     spread = (k_of_lane == lax.broadcasted_iota(jnp.int32, (16, 128), 0)).astype(BF16)
     masks = lax.dot_general(
@@ -88,7 +92,7 @@
     for q in range(4):
         projected = lax.dot_general(
             weight[...],
-            normed[q * 128 : (q + 1) * 128],
+            normed[q],
             (((0,), (1,)), ((), ())),
             preferred_element_type=F32,
         )
@@ -111,10 +115,13 @@
             for r in range(8):
                 target[pl.ds(z * 128 + r * 16, 16), :] = pieces[r].astype(BF16)
     for z in range(4):
-        block = pl.ds(z * 128, 128)
-        sent[block, :] = lax.dot_general(
-            right[block, :], left[...], (((1,), (1,)), ((), ())), preferred_element_type=F32
-        ).astype(BF16)
+        sums = lax.dot_general(
+            right[pl.ds(z * 128, 128), :],
+            left[...],
+            (((1,), (1,)), ((), ())),
+            preferred_element_type=F32,
+        )
+        sent[pl.ds((z % 2 * 2 + z // 2) * 128, 128), :] = sums.astype(BF16)
 
 
 def sum_kernel(got, sent, total, rows):
@@ -203,7 +210,7 @@
             pltpu.VMEM((1, 128), F32),
             pltpu.VMEM((1, 128), F32),
             pltpu.VMEM((1024, 128), F32),
-            pltpu.SemaphoreType.DMA((7,)),
+            pltpu.SemaphoreType.DMA((13,)),
         ],
         in_space=pltpu.HBM,
     )(*(pltpu.with_memory_space_constraint(a, pltpu.HBM) for a in inputs))
@@ -212,7 +219,7 @@
     partial = local_call(
         partial_kernel, shape((512, 512), BF16), [side, side, pltpu.VMEM((1024, 128), F32)]
     )(got.reshape(1024, 128))
-    parts = lax.all_to_all(partial.reshape(4, 128, 512), ("x1", "x0"), 0, 0, tiled=True)
+    parts = lax.all_to_all(partial.reshape(4, 128, 512), ("x0", "x1"), 0, 0, tiled=True)
     sums = local_call(
         sum_kernel,
         shape((512, 128), BF16),

time: 68.7 us -> 68.8 us (level)
  no operation moved by 1% of the time
where the time goes in v6:
time: 68.8 us; the launch traced here: 68.5 us
  blocking collectives  64.3 us (93%)
  Pallas kernels  4.18 us (6%)
    all_to_all x1, blocking collectives, on_device(): got = lax.all_to_all(sent.reshape(128, 8, 128), ORDER, 0, 0, tiled=True)  32.7 us
    all_to_all x1, blocking collectives, on_device(): back = lax.all_to_all(sums.reshape(128, 4, 128), ORDER, 0, 0, tiled=True)  19.1 us
    all_to_all x1, blocking collectives, on_device(): lax.all_to_all(partial.reshape(4, 128, 512), ('x0', 'x1'), 0, 0, tiled=True)  12.5 us
    pallas_call x4, Pallas kernels, call(): pl.pallas_call(kernel, out_shape=outs, in_specs=[pl.BlockSpec(memory_spac...  4.18 us

profile of v6, /device:TPU:1, one launch (start us, length us, event | category | flops | bytes accessed | tf_op | source)
XLA Modules:
  0.0 68.5 jit_solution(6580001153276250436)
XLA Ops:
  0.0 2.0 %shard_map.91 = (bf16[1024,128]{1,0:T(8,128)(2,1)S(1)}, bf16[512,128]{1,0:T(8,128)(2,1)S(1)}, f32[2,128]{1,0:T(2,128)S(1)}) custom-call(bf16[512,128]{1,0:T(8,128)(2,1)} %bitcast.19, bf16[128,512]{1,0:T(8,128)(2,1)} %weight_hbm.1, s32[16,32]{1,0:T(8,128)} %bitcast.20, f32[1,128]{1,0:T(1,128)} %bitcast.21, f32[1,128]{1,0:T(1,128)} %bitcast.22, ...), custom_call_target="tpu_custom_call" | custom-call | flops 1000000 | bytes 1048576 | tf_op jit(solution)/shard_map/pallas_call | solution.py:175
  2.0 32.7 %all_to_all.15 = bf16[128,8,128]{2,1,0:T(8,128)(2,1)S(1)} all-to-all(bf16[128,8,128]{2,1,0:T(8,128)(2,1)S(1)} %bitcast.18), channel_id=1, replica_groups=mesh['yh'=2,'z2'=2,'z1'=2,'z0'=2,'y1'=2,'y0'=2,'x1'=2,'x0'=2,'co'=2] {'y..., dimensions={0} | all-to-all | bytes 524288 | tf_op jit(solution)/shard_map/all_to_all | solution.py:217
  34.7 0.7 %shard_map.92 = bf16[512,512]{1,0:T(8,128)(2,1)S(1)} custom-call(bf16[1024,128]{1,0:T(8,128)(2,1)S(1)} %bitcast.15), custom_call_target="tpu_custom_call" | custom-call | flops 1000000 | bytes 1048576 | tf_op jit(solution)/shard_map/pallas_call | solution.py:175
  35.4 12.5 %all_to_all.16 = bf16[4,128,512]{2,1,0:T(8,128)(2,1)S(1)} all-to-all(bf16[4,128,512]{2,1,0:T(8,128)(2,1)S(1)} %bitcast.14), channel_id=1, replica_groups=mesh['yh'=2,'z2'=2,'z1'=2,'z0'=2,'y1'=2,'y0'=2,'x1'=2,'x0'=2,'co'=2] {'x..., dimensions={0} | all-to-all | bytes 1048576 | tf_op jit(solution)/shard_map/all_to_all | solution.py:222
  47.9 0.3 shard_map.93
  48.3 0.0 copy-start
  48.3 0.0 copy-start.1
  48.3 19.1 %all_to_all.17 = bf16[128,4,128]{2,1,0:T(4,128)(2,1)S(1)} all-to-all(bf16[128,4,128]{2,1,0:T(4,128)(2,1)S(1)} %bitcast.17), channel_id=1, replica_groups=mesh['yh'=2,'z2'=2,'z1'=2,'z0'=2,'y1'=2,'y0'=2,'x1'=2,'x0'=2,'co'=2] {'y..., dimensions={0} | all-to-all | bytes 262144 | tf_op jit(solution)/shard_map/all_to_all | solution.py:228
  67.4 0.0 copy-done
  67.4 0.0 copy-done.1
  67.4 1.1 %shard_map.94 = bf16[512,128]{1,0:T(8,128)(2,1)} custom-call(bf16[512,128]{1,0:T(8,128)(2,1)S(1)} %bitcast.16, bf16[512,128]{1,0:T(8,128)(2,1)S(1)} %get-tuple-element.9.normed, bf16[128,128]{1,0:T(8,128)(2,1)S(1)} %copy-done, f32[2,128]{1,0:T(2,128)S(1)} %get-tuple-element.10.scales, bf16[128,128]{1,0:T(8,128)(2,1)S(1)} %copy-done.1), custom_call_target="tpu_custom_call" | custom-call | flops 1000000 | bytes 1048576 | tf_op jit(solution)/shard_map/pallas_call | solution.py:175
Async XLA Ops:
  48.3 19.1 %copy-start = (bf16[128,128]{1,0:T(8,128)(2,1)S(1)}, bf16[128,128]{1,0:T(8,128)(2,1)}, u32[]{:S(2)}) copy-start(bf16[128,128]{1,0:T(8,128)(2,1)} %gate_weight.1) | copy-start | bytes 98308
  48.3 19.1 %copy-start.1 = (bf16[128,128]{1,0:T(8,128)(2,1)S(1)}, bf16[128,128]{1,0:T(8,128)(2,1)}, u32[]{:S(2)}) copy-start(bf16[128,128]{1,0:T(8,128)(2,1)} %out_weight.1) | copy-start | bytes 98308

commit v7 on v5

--- a/solution.py
+++ b/solution.py
@@ -9,6 +9,7 @@
 ROW_AXES = ("yh", "z2", "z1", "z0")
 COLUMN_AXES = ("y1", "y0", "x1", "x0", "co")
 ORDER = ("y1", "y0", "co", "z1", "z0", "yh", "z2")
+BACK_ORDER = ("y1", "y0", "z1", "z0", "yh", "z2")
 EPS = 1e-05
 F32 = jnp.float32
 BF16 = jnp.bfloat16
@@ -96,20 +97,27 @@
         rows[pl.ds(q * 2, 128, stride=8), :] = (
             jax.nn.sigmoid(projected[:128]) * projected[128:256] * keep
         )
-        rows[pl.ds(q * 2 + 1, 128, stride=8), :] = (
+        rows[pl.ds((q % 2 * 2 + q // 2) * 2 + 1, 128, stride=8), :] = (
             jax.nn.sigmoid(projected[256:384]) * projected[384:] * keep
         )
     sent[...] = rows[...].astype(BF16)
+
+
+def residues_in_lanes(rows, start, size, stride):
+    pieces = [rows[pl.ds(start + g * 128, size, stride=stride), :] for g in range(8)]
+    return swap_bits(pieces, ((0, 4), (1, 5), (2, 6)))
 
 
 def partial_kernel(got, sent, left, right, rows):
     rows[...] = got[...].astype(F32)
-    for side, target in enumerate((left, right)):
-        for z in range(4):
-            pieces = [rows[pl.ds(g * 128 + z * 32 + side, 16, stride=2), :] for g in range(8)]
-            pieces = swap_bits(pieces, ((0, 4), (1, 5), (2, 6)))
-            for r in range(8):
-                target[pl.ds(z * 128 + r * 16, 16), :] = pieces[r].astype(BF16)
+    for z in range(4):
+        for r, piece in enumerate(residues_in_lanes(rows, z * 32, 16, 2)):
+            left[pl.ds(z * 128 + r * 16, 16), :] = piece.astype(BF16)
+        for core in range(2):
+            pieces = residues_in_lanes(rows, z * 32 + core * 2 + 1, 8, 4)
+            for r in range(0, 8, 2):
+                both = jnp.concatenate(pieces[r : r + 2], axis=0)
+                right[pl.ds(z * 128 + core * 64 + r * 8, 16), :] = both.astype(BF16)
     for z in range(4):
         block = pl.ds(z * 128, 128)
         sent[block, :] = lax.dot_general(
@@ -118,16 +126,21 @@
 
 
 def sum_kernel(got, sent, total, rows):
-    for z in range(4):
-        lanes = pl.ds(z * 128, 128)
-        total[lanes, :] = sum(got[pl.ds(x * 128, 128), lanes].astype(F32) for x in range(4))
-        for jh in range(2):
-            pieces = [total[pl.ds(z * 128 + r * 16 + jh, 8, stride=2), :] for r in range(8)]
-            pieces = swap_bits(pieces, ((0, 2), (1, 3)))
-            for v in range(8):
-                at = (z * 4 + (v & 3)) * 4 + jh * 2 + (v >> 2)
-                rows[pl.ds(at, 8, stride=64), :] = pieces[v]
-    sent[...] = rows[...].astype(BF16)
+    for core in range(2):
+        for z in range(4):
+            base = (core * 4 + z) * 64
+            total[pl.ds(base, 64), :] = sum(
+                got[pl.ds((x * 2 + core) * 64, 64), pl.ds(z * 128, 128)].astype(F32)
+                for x in range(4)
+            )
+            for jh in range(2):
+                pieces = [total[pl.ds(base + t * 16 + jh, 8, stride=2), :] for t in range(4)]
+                pieces = swap_bits(pieces, ((0, 2), (1, 3)))
+                for v in range(4):
+                    for low in range(2):
+                        at = (z * 4 + v) * 8 + core * 4 + jh * 2 + low
+                        rows[pl.ds(at, 4, stride=128), :] = pieces[v][low * 4 : low * 4 + 4]
+    sent[...] = rows[0:512, :].astype(BF16)
 
 
 def mix_kernel(
@@ -137,7 +150,14 @@
     gains = jnp.broadcast_to(scales[0:1, :], (128, 128)).T
     biases = jnp.broadcast_to(scales[1:2, :], (128, 128)).T
     for h in range(4):
-        triangle = rows[pl.ds(h, 128, stride=4), :]
+        triangle = jnp.concatenate(
+            [
+                rows[pl.ds(y * 128 + core * 4 + h, 16, stride=8), :]
+                for y in range(4)
+                for core in range(2)
+            ],
+            axis=0,
+        )
         centered = triangle - jnp.mean(triangle, axis=0, keepdims=True)
         variance = jnp.mean(centered * centered, axis=0, keepdims=True)
         tri_normed = (centered * lax.rsqrt(variance + EPS) * gains + biases).astype(BF16)
@@ -152,7 +172,8 @@
         )
         for h in range(4):
             for jj in range(4):
-                ordered[pl.ds(s * 128 + h * 4 + jj, 8, stride=16), :] = mixed[
+                column = h // 2 * 8 + jj * 2 + h % 2
+                ordered[pl.ds(s * 128 + column, 8, stride=16), :] = mixed[
                     pl.ds(h * 128 + jj * 4 + s, 8, stride=16), :
                 ]
         staged[block, :] = (ordered[block, :] * gating).astype(BF16)
@@ -212,13 +233,13 @@
     partial = local_call(
         partial_kernel, shape((512, 512), BF16), [side, side, pltpu.VMEM((1024, 128), F32)]
     )(got.reshape(1024, 128))
-    parts = lax.all_to_all(partial.reshape(4, 128, 512), ("x1", "x0"), 0, 0, tiled=True)
+    parts = lax.all_to_all(partial.reshape(8, 64, 512), ("x1", "x0", "co"), 0, 0, tiled=True)
     sums = local_call(
         sum_kernel,
         shape((512, 128), BF16),
-        [pltpu.VMEM((512, 128), F32), pltpu.VMEM((512, 128), F32)],
+        [pltpu.VMEM((512, 128), F32), pltpu.VMEM((1024, 128), F32)],
     )(parts.reshape(512, 512))
-    back = lax.all_to_all(sums.reshape(128, 4, 128), ORDER, 0, 0, tiled=True)
+    back = lax.all_to_all(sums.reshape(64, 8, 128), BACK_ORDER, 0, 0, tiled=True)
     block = pltpu.VMEM((512, 128), F32)
     update = local_call(
         mix_kernel,

time: 68.7 us -> 66.6 us (0.969)
  blocking collectives: 64.6 us -> 62 us
    all_to_all x2, blocking collectives: 31.9 us -> 29.2 us  [the longest x1 15.6 us: on_device(): lax.all_to_all(sums.reshape(64, 8, 128), BACK_ORDER, 0, 0, tiled=True)]
where the time goes in v7:
time: 66.6 us; the launch traced here: 65.8 us
  blocking collectives  62 us (93%)
  Pallas kernels  3.77 us (6%)
    all_to_all x1, blocking collectives, on_device(): got = lax.all_to_all(sent.reshape(128, 8, 128), ORDER, 0, 0, tiled=True)  32.7 us
    all_to_all x1, blocking collectives, on_device(): lax.all_to_all(sums.reshape(64, 8, 128), BACK_ORDER, 0, 0, tiled=True)  15.6 us
    all_to_all x1, blocking collectives, on_device(): lax.all_to_all(partial.reshape(8, 64, 512), ('x1', 'x0', 'co'), 0, 0, til...  13.6 us
    pallas_call x4, Pallas kernels, call(): pl.pallas_call(kernel, out_shape=outs, in_specs=[pl.BlockSpec(memory_spac...  3.77 us

profile of v7, /device:TPU:1, one launch (start us, length us, event | category | flops | bytes accessed | tf_op | source)
XLA Modules:
  0.0 65.8 jit_solution(1833055895681492028)
XLA Ops:
  0.0 1.6 %shard_map.91 = (bf16[1024,128]{1,0:T(8,128)(2,1)S(1)}, bf16[512,128]{1,0:T(8,128)(2,1)S(1)}, f32[2,128]{1,0:T(2,128)S(1)}) custom-call(bf16[512,128]{1,0:T(8,128)(2,1)} %bitcast.19, bf16[128,512]{1,0:T(8,128)(2,1)} %weight_hbm.1, s32[16,32]{1,0:T(8,128)} %bitcast.20, f32[1,128]{1,0:T(1,128)} %bitcast.21, f32[1,128]{1,0:T(1,128)} %bitcast.22, ...), custom_call_target="tpu_custom_call" | custom-call | flops 1000000 | bytes 1048576 | tf_op jit(solution)/shard_map/pallas_call | solution.py:189
  1.6 32.7 %all_to_all.15 = bf16[128,8,128]{2,1,0:T(8,128)(2,1)S(1)} all-to-all(bf16[128,8,128]{2,1,0:T(8,128)(2,1)S(1)} %bitcast.18), channel_id=1, replica_groups=mesh['yh'=2,'z2'=2,'z1'=2,'z0'=2,'y1'=2,'y0'=2,'x1'=2,'x0'=2,'co'=2] {'y..., dimensions={0} | all-to-all | bytes 524288 | tf_op jit(solution)/shard_map/all_to_all | solution.py:231
  34.3 0.7 %shard_map.92 = bf16[512,512]{1,0:T(8,128)(2,1)S(1)} custom-call(bf16[1024,128]{1,0:T(8,128)(2,1)S(1)} %bitcast.15), custom_call_target="tpu_custom_call" | custom-call | flops 1000000 | bytes 1048576 | tf_op jit(solution)/shard_map/pallas_call | solution.py:189
  35.0 13.6 %all_to_all.16 = bf16[8,64,512]{2,1,0:T(8,128)(2,1)S(1)} all-to-all(bf16[8,64,512]{2,1,0:T(8,128)(2,1)S(1)} %bitcast.14), channel_id=1, replica_groups=mesh['yh'=2,'z2'=2,'z1'=2,'z0'=2,'y1'=2,'y0'=2,'x1'=2,'x0'=2,'co'=2] {'x..., dimensions={0} | all-to-all | bytes 1048576 | tf_op jit(solution)/shard_map/all_to_all | solution.py:236
  48.6 0.3 shard_map.93
  49.0 0.0 copy-start
  49.0 0.0 copy-start.1
  49.0 15.6 %all_to_all.17 = bf16[64,8,128]{2,1,0:T(8,128)(2,1)S(1)} all-to-all(bf16[64,8,128]{2,1,0:T(8,128)(2,1)S(1)} %bitcast.17), channel_id=1, replica_groups=mesh['yh'=2,'z2'=2,'z1'=2,'z0'=2,'y1'=2,'y0'=2,'x1'=2,'x0'=2,'co'=2] {'y..., dimensions={0} | all-to-all | bytes 262144 | tf_op jit(solution)/shard_map/all_to_all | solution.py:242
  64.6 0.0 copy-done
  64.6 0.0 copy-done.1
  64.6 1.1 %shard_map.94 = bf16[512,128]{1,0:T(8,128)(2,1)} custom-call(bf16[512,128]{1,0:T(8,128)(2,1)S(1)} %bitcast.16, bf16[512,128]{1,0:T(8,128)(2,1)S(1)} %get-tuple-element.9.normed, bf16[128,128]{1,0:T(8,128)(2,1)S(1)} %copy-done, f32[2,128]{1,0:T(2,128)S(1)} %get-tuple-element.10.scales, bf16[128,128]{1,0:T(8,128)(2,1)S(1)} %copy-done.1), custom_call_target="tpu_custom_call" | custom-call | flops 1000000 | bytes 1048576 | tf_op jit(solution)/shard_map/pallas_call | solution.py:189
Async XLA Ops:
  49.0 15.6 %copy-start = (bf16[128,128]{1,0:T(8,128)(2,1)S(1)}, bf16[128,128]{1,0:T(8,128)(2,1)}, u32[]{:S(2)}) copy-start(bf16[128,128]{1,0:T(8,128)(2,1)} %gate_weight.1) | copy-start | bytes 98308
  49.0 15.6 %copy-start.1 = (bf16[128,128]{1,0:T(8,128)(2,1)S(1)}, bf16[128,128]{1,0:T(8,128)(2,1)}, u32[]{:S(2)}) copy-start(bf16[128,128]{1,0:T(8,128)(2,1)} %out_weight.1) | copy-start | bytes 98308

commit v8 on v7

--- a/solution.py
+++ b/solution.py
@@ -53,11 +53,12 @@
     rows,
     sems,
 ):
+    halves = [(pl.ds(h * 256, 256), pl.ds(h * 64, 64)) for h in range(2)]
     moves = (
-        (pair_hbm, pair),
+        *((pair_hbm.at[h], pair.at[h]) for h, _ in halves),
+        *((weight_hbm.at[h], weight.at[h]) for _, h in halves),
         (gain_hbm, gain),
         (bias_hbm, bias),
-        (weight_hbm, weight),
         (mask_hbm, mask),
         (out_gain_hbm, scales.at[pl.ds(0, 1)]),
         (out_bias_hbm, scales.at[pl.ds(1, 1)]),
@@ -69,11 +70,12 @@
     for copy in copies:
         copy.start()
     copies[0].wait()
+    copies[1].wait()
     x = pair[...].astype(F32)
     centered = x - jnp.mean(x, axis=-1, keepdims=True)
     variance = jnp.mean(centered * centered, axis=-1, keepdims=True)
     normalized = centered * lax.rsqrt(variance + EPS)
-    for copy in copies[1:]:
+    for copy in copies[2:]:
         copy.wait()
     normed = (normalized * gain[...] + bias[...]).astype(BF16)
     normed_out[...] = normed
@@ -119,10 +121,15 @@
                 both = jnp.concatenate(pieces[r : r + 2], axis=0)
                 right[pl.ds(z * 128 + core * 64 + r * 8, 16), :] = both.astype(BF16)
     for z in range(4):
-        block = pl.ds(z * 128, 128)
-        sent[block, :] = lax.dot_general(
-            right[block, :], left[...], (((1,), (1,)), ((), ())), preferred_element_type=F32
+        sums = lax.dot_general(
+            right[pl.ds(z * 128, 128), :],
+            left[...],
+            (((1,), (1,)), ((), ())),
+            preferred_element_type=F32,
         ).astype(BF16)
+        for core in range(2):
+            to = (core * 4 + z % 2 * 2 + z // 2) * 64
+            sent[pl.ds(to, 64), :] = sums[core * 64 : core * 64 + 64]
 
 
 def sum_kernel(got, sent, total, rows):
@@ -130,7 +137,7 @@
         for z in range(4):
             base = (core * 4 + z) * 64
             total[pl.ds(base, 64), :] = sum(
-                got[pl.ds((x * 2 + core) * 64, 64), pl.ds(z * 128, 128)].astype(F32)
+                got[pl.ds((core * 4 + x) * 64, 64), pl.ds(z * 128, 128)].astype(F32)
                 for x in range(4)
             )
             for jh in range(2):
@@ -224,7 +231,7 @@
             pltpu.VMEM((1, 128), F32),
             pltpu.VMEM((1, 128), F32),
             pltpu.VMEM((1024, 128), F32),
-            pltpu.SemaphoreType.DMA((7,)),
+            pltpu.SemaphoreType.DMA((9,)),
         ],
         in_space=pltpu.HBM,
     )(*(pltpu.with_memory_space_constraint(a, pltpu.HBM) for a in inputs))
@@ -233,7 +240,7 @@
     partial = local_call(
         partial_kernel, shape((512, 512), BF16), [side, side, pltpu.VMEM((1024, 128), F32)]
     )(got.reshape(1024, 128))
-    parts = lax.all_to_all(partial.reshape(8, 64, 512), ("x1", "x0", "co"), 0, 0, tiled=True)
+    parts = lax.all_to_all(partial.reshape(8, 64, 512), ("co", "x0", "x1"), 0, 0, tiled=True)
     sums = local_call(
         sum_kernel,
         shape((512, 128), BF16),

time: 66.6 us -> 66.3 us (level)
  no operation moved by 1% of the time
where the time goes in v8:
time: 66.3 us; the launch traced here: 66 us
  blocking collectives  62.2 us (94%)
  Pallas kernels  3.76 us (6%)
    all_to_all x1, blocking collectives, on_device(): got = lax.all_to_all(sent.reshape(128, 8, 128), ORDER, 0, 0, tiled=True)  32.7 us
    all_to_all x1, blocking collectives, on_device(): lax.all_to_all(sums.reshape(64, 8, 128), BACK_ORDER, 0, 0, tiled=True)  15.8 us
    all_to_all x1, blocking collectives, on_device(): lax.all_to_all(partial.reshape(8, 64, 512), ('co', 'x0', 'x1'), 0, 0, til...  13.6 us
    pallas_call x4, Pallas kernels, call(): pl.pallas_call(kernel, out_shape=outs, in_specs=[pl.BlockSpec(memory_spac...  3.76 us

profile of v8, /device:TPU:1, one launch (start us, length us, event | category | flops | bytes accessed | tf_op | source)
XLA Modules:
  0.0 66.0 jit_solution(10728873233037380350)
XLA Ops:
  0.0 1.6 %shard_map.91 = (bf16[1024,128]{1,0:T(8,128)(2,1)S(1)}, bf16[512,128]{1,0:T(8,128)(2,1)S(1)}, f32[2,128]{1,0:T(2,128)S(1)}) custom-call(bf16[512,128]{1,0:T(8,128)(2,1)} %bitcast.19, bf16[128,512]{1,0:T(8,128)(2,1)} %weight_hbm.1, s32[16,32]{1,0:T(8,128)} %bitcast.20, f32[1,128]{1,0:T(1,128)} %bitcast.21, f32[1,128]{1,0:T(1,128)} %bitcast.22, ...), custom_call_target="tpu_custom_call" | custom-call | flops 1000000 | bytes 1048576 | tf_op jit(solution)/shard_map/pallas_call | solution.py:196
  1.6 32.7 %all_to_all.15 = bf16[128,8,128]{2,1,0:T(8,128)(2,1)S(1)} all-to-all(bf16[128,8,128]{2,1,0:T(8,128)(2,1)S(1)} %bitcast.18), channel_id=1, replica_groups=mesh['yh'=2,'z2'=2,'z1'=2,'z0'=2,'y1'=2,'y0'=2,'x1'=2,'x0'=2,'co'=2] {'y..., dimensions={0} | all-to-all | bytes 524288 | tf_op jit(solution)/shard_map/all_to_all | solution.py:238
  34.3 0.7 %shard_map.92 = bf16[512,512]{1,0:T(8,128)(2,1)S(1)} custom-call(bf16[1024,128]{1,0:T(8,128)(2,1)S(1)} %bitcast.15), custom_call_target="tpu_custom_call" | custom-call | flops 1000000 | bytes 1048576 | tf_op jit(solution)/shard_map/pallas_call | solution.py:196
  35.0 13.6 %all_to_all.16 = bf16[8,64,512]{2,1,0:T(8,128)(2,1)S(1)} all-to-all(bf16[8,64,512]{2,1,0:T(8,128)(2,1)S(1)} %bitcast.14), channel_id=1, replica_groups=mesh['yh'=2,'z2'=2,'z1'=2,'z0'=2,'y1'=2,'y0'=2,'x1'=2,'x0'=2,'co'=2] {'c..., dimensions={0} | all-to-all | bytes 1048576 | tf_op jit(solution)/shard_map/all_to_all | solution.py:243
  48.6 0.3 shard_map.93
  49.0 0.0 copy-start
  49.0 0.0 copy-start.1
  49.0 15.8 %all_to_all.17 = bf16[64,8,128]{2,1,0:T(8,128)(2,1)S(1)} all-to-all(bf16[64,8,128]{2,1,0:T(8,128)(2,1)S(1)} %bitcast.17), channel_id=1, replica_groups=mesh['yh'=2,'z2'=2,'z1'=2,'z0'=2,'y1'=2,'y0'=2,'x1'=2,'x0'=2,'co'=2] {'y..., dimensions={0} | all-to-all | bytes 262144 | tf_op jit(solution)/shard_map/all_to_all | solution.py:249
  64.8 0.0 copy-done
  64.8 0.0 copy-done.1
  64.8 1.1 %shard_map.94 = bf16[512,128]{1,0:T(8,128)(2,1)} custom-call(bf16[512,128]{1,0:T(8,128)(2,1)S(1)} %bitcast.16, bf16[512,128]{1,0:T(8,128)(2,1)S(1)} %get-tuple-element.9.normed, bf16[128,128]{1,0:T(8,128)(2,1)S(1)} %copy-done, f32[2,128]{1,0:T(2,128)S(1)} %get-tuple-element.10.scales, bf16[128,128]{1,0:T(8,128)(2,1)S(1)} %copy-done.1), custom_call_target="tpu_custom_call" | custom-call | flops 1000000 | bytes 1048576 | tf_op jit(solution)/shard_map/pallas_call | solution.py:196
Async XLA Ops:
  49.0 15.9 %copy-start = (bf16[128,128]{1,0:T(8,128)(2,1)S(1)}, bf16[128,128]{1,0:T(8,128)(2,1)}, u32[]{:S(2)}) copy-start(bf16[128,128]{1,0:T(8,128)(2,1)} %gate_weight.1) | copy-start | bytes 98308
  49.0 15.9 %copy-start.1 = (bf16[128,128]{1,0:T(8,128)(2,1)S(1)}, bf16[128,128]{1,0:T(8,128)(2,1)}, u32[]{:S(2)}) copy-start(bf16[128,128]{1,0:T(8,128)(2,1)} %out_weight.1) | copy-start | bytes 98308

commit v9 on v7

--- a/solution.py
+++ b/solution.py
@@ -8,7 +8,7 @@
 
 ROW_AXES = ("yh", "z2", "z1", "z0")
 COLUMN_AXES = ("y1", "y0", "x1", "x0", "co")
-ORDER = ("y1", "y0", "co", "z1", "z0", "yh", "z2")
+ORDER = ("y1", "y0", "x0", "z1", "z0", "yh", "z2")
 BACK_ORDER = ("y1", "y0", "z1", "z0", "yh", "z2")
 EPS = 1e-05
 F32 = jnp.float32
@@ -126,19 +126,20 @@
 
 
 def sum_kernel(got, sent, total, rows):
-    for core in range(2):
+    for x0 in range(2):
         for z in range(4):
-            base = (core * 4 + z) * 64
+            base = (x0 * 4 + z) * 64
             total[pl.ds(base, 64), :] = sum(
-                got[pl.ds((x * 2 + core) * 64, 64), pl.ds(z * 128, 128)].astype(F32)
-                for x in range(4)
+                got[pl.ds((x1 * 4 + x0 * 2 + core) * 64, 64), pl.ds(z * 128, 128)].astype(F32)
+                for x1 in range(2)
+                for core in range(2)
             )
             for jh in range(2):
                 pieces = [total[pl.ds(base + t * 16 + jh, 8, stride=2), :] for t in range(4)]
                 pieces = swap_bits(pieces, ((0, 2), (1, 3)))
                 for v in range(4):
                     for low in range(2):
-                        at = (z * 4 + v) * 8 + core * 4 + jh * 2 + low
+                        at = (z * 4 + v) * 8 + x0 * 4 + jh * 2 + low
                         rows[pl.ds(at, 4, stride=128), :] = pieces[v][low * 4 : low * 4 + 4]
     sent[...] = rows[0:512, :].astype(BF16)
 
@@ -152,9 +153,9 @@
     for h in range(4):
         triangle = jnp.concatenate(
             [
-                rows[pl.ds(y * 128 + core * 4 + h, 16, stride=8), :]
+                rows[pl.ds(y * 128 + x0 * 4 + h, 16, stride=8), :]
                 for y in range(4)
-                for core in range(2)
+                for x0 in range(2)
             ],
             axis=0,
         )

time: 66.6 us -> 67.2 us (level)
    all_to_all x1, blocking collectives: 13.6 us -> 16 us  [on_device(): lax.all_to_all(partial.reshape(8, 64, 512), ('x1', 'x0', 'co'), 0, 0, til...]
    all_to_all x1, blocking collectives: 32.7 us -> 31.4 us  [on_device(): got = lax.all_to_all(sent.reshape(128, 8, 128), ORDER, 0, 0, tiled=True)]
where the time goes in v9:
time: 67.2 us; the launch traced here: 66.4 us
  blocking collectives  62.6 us (93%)
  Pallas kernels  3.77 us (6%)
    all_to_all x1, blocking collectives, on_device(): got = lax.all_to_all(sent.reshape(128, 8, 128), ORDER, 0, 0, tiled=True)  31.4 us
    all_to_all x1, blocking collectives, on_device(): lax.all_to_all(partial.reshape(8, 64, 512), ('x1', 'x0', 'co'), 0, 0, til...  16 us
    all_to_all x1, blocking collectives, on_device(): lax.all_to_all(sums.reshape(64, 8, 128), BACK_ORDER, 0, 0, tiled=True)  15.2 us
    pallas_call x4, Pallas kernels, call(): pl.pallas_call(kernel, out_shape=outs, in_specs=[pl.BlockSpec(memory_spac...  3.77 us

profile of v9, /device:TPU:1, one launch (start us, length us, event | category | flops | bytes accessed | tf_op | source)
XLA Modules:
  0.0 66.4 jit_solution(16373739164879504345)
XLA Ops:
  0.0 1.6 %shard_map.91 = (bf16[1024,128]{1,0:T(8,128)(2,1)S(1)}, bf16[512,128]{1,0:T(8,128)(2,1)S(1)}, f32[2,128]{1,0:T(2,128)S(1)}) custom-call(bf16[512,128]{1,0:T(8,128)(2,1)} %bitcast.19, bf16[128,512]{1,0:T(8,128)(2,1)} %weight_hbm.1, s32[16,32]{1,0:T(8,128)} %bitcast.20, f32[1,128]{1,0:T(1,128)} %bitcast.21, f32[1,128]{1,0:T(1,128)} %bitcast.22, ...), custom_call_target="tpu_custom_call" | custom-call | flops 1000000 | bytes 1048576 | tf_op jit(solution)/shard_map/pallas_call | solution.py:190
  1.6 31.4 %all_to_all.15 = bf16[128,8,128]{2,1,0:T(8,128)(2,1)S(1)} all-to-all(bf16[128,8,128]{2,1,0:T(8,128)(2,1)S(1)} %bitcast.18), channel_id=1, replica_groups=mesh['yh'=2,'z2'=2,'z1'=2,'z0'=2,'y1'=2,'y0'=2,'x1'=2,'x0'=2,'co'=2] {'y..., dimensions={0} | all-to-all | bytes 524288 | tf_op jit(solution)/shard_map/all_to_all | solution.py:232
  33.0 0.7 %shard_map.92 = bf16[512,512]{1,0:T(8,128)(2,1)S(1)} custom-call(bf16[1024,128]{1,0:T(8,128)(2,1)S(1)} %bitcast.15), custom_call_target="tpu_custom_call" | custom-call | flops 1000000 | bytes 1048576 | tf_op jit(solution)/shard_map/pallas_call | solution.py:190
  33.7 16.0 %all_to_all.16 = bf16[8,64,512]{2,1,0:T(8,128)(2,1)S(1)} all-to-all(bf16[8,64,512]{2,1,0:T(8,128)(2,1)S(1)} %bitcast.14), channel_id=1, replica_groups=mesh['yh'=2,'z2'=2,'z1'=2,'z0'=2,'y1'=2,'y0'=2,'x1'=2,'x0'=2,'co'=2] {'x..., dimensions={0} | all-to-all | bytes 1048576 | tf_op jit(solution)/shard_map/all_to_all | solution.py:237
  49.8 0.3 shard_map.93
  50.1 0.0 copy-start
  50.1 0.0 copy-start.1
  50.1 15.2 %all_to_all.17 = bf16[64,8,128]{2,1,0:T(8,128)(2,1)S(1)} all-to-all(bf16[64,8,128]{2,1,0:T(8,128)(2,1)S(1)} %bitcast.17), channel_id=1, replica_groups=mesh['yh'=2,'z2'=2,'z1'=2,'z0'=2,'y1'=2,'y0'=2,'x1'=2,'x0'=2,'co'=2] {'y..., dimensions={0} | all-to-all | bytes 262144 | tf_op jit(solution)/shard_map/all_to_all | solution.py:243
  65.3 0.0 copy-done
  65.3 0.0 copy-done.1
  65.3 1.1 %shard_map.94 = bf16[512,128]{1,0:T(8,128)(2,1)} custom-call(bf16[512,128]{1,0:T(8,128)(2,1)S(1)} %bitcast.16, bf16[512,128]{1,0:T(8,128)(2,1)S(1)} %get-tuple-element.9.normed, bf16[128,128]{1,0:T(8,128)(2,1)S(1)} %copy-done, f32[2,128]{1,0:T(2,128)S(1)} %get-tuple-element.10.scales, bf16[128,128]{1,0:T(8,128)(2,1)S(1)} %copy-done.1), custom_call_target="tpu_custom_call" | custom-call | flops 1000000 | bytes 1048576 | tf_op jit(solution)/shard_map/pallas_call | solution.py:190
Async XLA Ops:
  50.1 15.2 %copy-start = (bf16[128,128]{1,0:T(8,128)(2,1)S(1)}, bf16[128,128]{1,0:T(8,128)(2,1)}, u32[]{:S(2)}) copy-start(bf16[128,128]{1,0:T(8,128)(2,1)} %gate_weight.1) | copy-start | bytes 98308
  50.1 15.2 %copy-start.1 = (bf16[128,128]{1,0:T(8,128)(2,1)S(1)}, bf16[128,128]{1,0:T(8,128)(2,1)}, u32[]{:S(2)}) copy-start(bf16[128,128]{1,0:T(8,128)(2,1)} %out_weight.1) | copy-start | bytes 98308

commit v10 on v7

--- a/solution.py
+++ b/solution.py
@@ -8,8 +8,8 @@
 
 ROW_AXES = ("yh", "z2", "z1", "z0")
 COLUMN_AXES = ("y1", "y0", "x1", "x0", "co")
-ORDER = ("y1", "y0", "co", "z1", "z0", "yh", "z2")
-BACK_ORDER = ("y1", "y0", "z1", "z0", "yh", "z2")
+ORDER = ("y0", "y1", "co", "z1", "z0", "z2", "yh")
+BACK_ORDER = ("y0", "y1", "z1", "z0", "z2", "yh")
 EPS = 1e-05
 F32 = jnp.float32
 BF16 = jnp.bfloat16

time: 66.6 us -> 66.6 us (level)
  no operation moved by 1% of the time
where the time goes in v10:
time: 66.6 us; the launch traced here: 65.8 us
  blocking collectives  62 us (93%)
  Pallas kernels  3.77 us (6%)
    all_to_all x1, blocking collectives, on_device(): got = lax.all_to_all(sent.reshape(128, 8, 128), ORDER, 0, 0, tiled=True)  32.7 us
    all_to_all x1, blocking collectives, on_device(): lax.all_to_all(sums.reshape(64, 8, 128), BACK_ORDER, 0, 0, tiled=True)  15.7 us
    all_to_all x1, blocking collectives, on_device(): lax.all_to_all(partial.reshape(8, 64, 512), ('x1', 'x0', 'co'), 0, 0, til...  13.5 us
    pallas_call x4, Pallas kernels, call(): pl.pallas_call(kernel, out_shape=outs, in_specs=[pl.BlockSpec(memory_spac...  3.77 us

profile of v10, /device:TPU:1, one launch (start us, length us, event | category | flops | bytes accessed | tf_op | source)
XLA Modules:
  0.0 65.8 jit_solution(10174355403266301942)
XLA Ops:
  0.0 1.6 %shard_map.91 = (bf16[1024,128]{1,0:T(8,128)(2,1)S(1)}, bf16[512,128]{1,0:T(8,128)(2,1)S(1)}, f32[2,128]{1,0:T(2,128)S(1)}) custom-call(bf16[512,128]{1,0:T(8,128)(2,1)} %bitcast.19, bf16[128,512]{1,0:T(8,128)(2,1)} %weight_hbm.1, s32[16,32]{1,0:T(8,128)} %bitcast.20, f32[1,128]{1,0:T(1,128)} %bitcast.21, f32[1,128]{1,0:T(1,128)} %bitcast.22, ...), custom_call_target="tpu_custom_call" | custom-call | flops 1000000 | bytes 1048576 | tf_op jit(solution)/shard_map/pallas_call | solution.py:189
  1.6 32.7 %all_to_all.15 = bf16[128,8,128]{2,1,0:T(8,128)(2,1)S(1)} all-to-all(bf16[128,8,128]{2,1,0:T(8,128)(2,1)S(1)} %bitcast.18), channel_id=1, replica_groups=mesh['yh'=2,'z2'=2,'z1'=2,'z0'=2,'y1'=2,'y0'=2,'x1'=2,'x0'=2,'co'=2] {'y..., dimensions={0} | all-to-all | bytes 524288 | tf_op jit(solution)/shard_map/all_to_all | solution.py:231
  34.3 0.7 %shard_map.92 = bf16[512,512]{1,0:T(8,128)(2,1)S(1)} custom-call(bf16[1024,128]{1,0:T(8,128)(2,1)S(1)} %bitcast.15), custom_call_target="tpu_custom_call" | custom-call | flops 1000000 | bytes 1048576 | tf_op jit(solution)/shard_map/pallas_call | solution.py:189
  35.0 13.5 %all_to_all.16 = bf16[8,64,512]{2,1,0:T(8,128)(2,1)S(1)} all-to-all(bf16[8,64,512]{2,1,0:T(8,128)(2,1)S(1)} %bitcast.14), channel_id=1, replica_groups=mesh['yh'=2,'z2'=2,'z1'=2,'z0'=2,'y1'=2,'y0'=2,'x1'=2,'x0'=2,'co'=2] {'x..., dimensions={0} | all-to-all | bytes 1048576 | tf_op jit(solution)/shard_map/all_to_all | solution.py:236
  48.5 0.3 shard_map.93
  48.9 0.0 copy-start
  48.9 0.0 copy-start.1
  48.9 15.7 %all_to_all.17 = bf16[64,8,128]{2,1,0:T(8,128)(2,1)S(1)} all-to-all(bf16[64,8,128]{2,1,0:T(8,128)(2,1)S(1)} %bitcast.17), channel_id=1, replica_groups=mesh['yh'=2,'z2'=2,'z1'=2,'z0'=2,'y1'=2,'y0'=2,'x1'=2,'x0'=2,'co'=2] {'y..., dimensions={0} | all-to-all | bytes 262144 | tf_op jit(solution)/shard_map/all_to_all | solution.py:242
  64.6 0.0 copy-done
  64.6 0.0 copy-done.1
  64.6 1.1 %shard_map.94 = bf16[512,128]{1,0:T(8,128)(2,1)} custom-call(bf16[512,128]{1,0:T(8,128)(2,1)S(1)} %bitcast.16, bf16[512,128]{1,0:T(8,128)(2,1)S(1)} %get-tuple-element.9.normed, bf16[128,128]{1,0:T(8,128)(2,1)S(1)} %copy-done, f32[2,128]{1,0:T(2,128)S(1)} %get-tuple-element.10.scales, bf16[128,128]{1,0:T(8,128)(2,1)S(1)} %copy-done.1), custom_call_target="tpu_custom_call" | custom-call | flops 1000000 | bytes 1048576 | tf_op jit(solution)/shard_map/pallas_call | solution.py:189
Async XLA Ops:
  48.9 15.8 %copy-start = (bf16[128,128]{1,0:T(8,128)(2,1)S(1)}, bf16[128,128]{1,0:T(8,128)(2,1)}, u32[]{:S(2)}) copy-start(bf16[128,128]{1,0:T(8,128)(2,1)} %gate_weight.1) | copy-start | bytes 98308
  48.9 15.8 %copy-start.1 = (bf16[128,128]{1,0:T(8,128)(2,1)S(1)}, bf16[128,128]{1,0:T(8,128)(2,1)}, u32[]{:S(2)}) copy-start(bf16[128,128]{1,0:T(8,128)(2,1)} %out_weight.1) | copy-start | bytes 98308

commit v11 on v7

--- a/solution.py
+++ b/solution.py
@@ -108,20 +108,19 @@
     return swap_bits(pieces, ((0, 4), (1, 5), (2, 6)))
 
 
-def partial_kernel(got, sent, left, right, rows):
+def partial_kernel(got, sent, left, rows):
     rows[...] = got[...].astype(F32)
     for z in range(4):
         for r, piece in enumerate(residues_in_lanes(rows, z * 32, 16, 2)):
             left[pl.ds(z * 128 + r * 16, 16), :] = piece.astype(BF16)
-        for core in range(2):
-            pieces = residues_in_lanes(rows, z * 32 + core * 2 + 1, 8, 4)
-            for r in range(0, 8, 2):
-                both = jnp.concatenate(pieces[r : r + 2], axis=0)
-                right[pl.ds(z * 128 + core * 64 + r * 8, 16), :] = both.astype(BF16)
     for z in range(4):
-        block = pl.ds(z * 128, 128)
-        sent[block, :] = lax.dot_general(
-            right[block, :], left[...], (((1,), (1,)), ((), ())), preferred_element_type=F32
+        pieces = [
+            *residues_in_lanes(rows, z * 32 + 1, 8, 4),
+            *residues_in_lanes(rows, z * 32 + 3, 8, 4),
+        ]
+        right = jnp.concatenate(pieces, axis=0).astype(BF16)
+        sent[pl.ds(z * 128, 128), :] = lax.dot_general(
+            right, left[...], (((1,), (1,)), ((), ())), preferred_element_type=F32
         ).astype(BF16)
 
 
@@ -231,7 +230,7 @@
     got = lax.all_to_all(sent.reshape(128, 8, 128), ORDER, 0, 0, tiled=True)
     side = pltpu.VMEM((512, 128), BF16)
     partial = local_call(
-        partial_kernel, shape((512, 512), BF16), [side, side, pltpu.VMEM((1024, 128), F32)]
+        partial_kernel, shape((512, 512), BF16), [side, pltpu.VMEM((1024, 128), F32)]
     )(got.reshape(1024, 128))
     parts = lax.all_to_all(partial.reshape(8, 64, 512), ("x1", "x0", "co"), 0, 0, tiled=True)
     sums = local_call(

time: 66.6 us -> 66.6 us (level)
  no operation moved by 1% of the time
where the time goes in v11:
time: 66.6 us; the launch traced here: 65.8 us
  blocking collectives  62 us (93%)
  Pallas kernels  3.75 us (6%)
    all_to_all x1, blocking collectives, on_device(): got = lax.all_to_all(sent.reshape(128, 8, 128), ORDER, 0, 0, tiled=True)  32.7 us
    all_to_all x1, blocking collectives, on_device(): lax.all_to_all(sums.reshape(64, 8, 128), BACK_ORDER, 0, 0, tiled=True)  15.6 us
    all_to_all x1, blocking collectives, on_device(): lax.all_to_all(partial.reshape(8, 64, 512), ('x1', 'x0', 'co'), 0, 0, til...  13.6 us
    pallas_call x4, Pallas kernels, call(): pl.pallas_call(kernel, out_shape=outs, in_specs=[pl.BlockSpec(memory_spac...  3.75 us

profile of v11, /device:TPU:1, one launch (start us, length us, event | category | flops | bytes accessed | tf_op | source)
XLA Modules:
  0.0 65.8 jit_solution(4881391352183791248)
XLA Ops:
  0.0 1.6 %shard_map.91 = (bf16[1024,128]{1,0:T(8,128)(2,1)S(1)}, bf16[512,128]{1,0:T(8,128)(2,1)S(1)}, f32[2,128]{1,0:T(2,128)S(1)}) custom-call(bf16[512,128]{1,0:T(8,128)(2,1)} %bitcast.19, bf16[128,512]{1,0:T(8,128)(2,1)} %weight_hbm.1, s32[16,32]{1,0:T(8,128)} %bitcast.20, f32[1,128]{1,0:T(1,128)} %bitcast.21, f32[1,128]{1,0:T(1,128)} %bitcast.22, ...), custom_call_target="tpu_custom_call" | custom-call | flops 1000000 | bytes 1048576 | tf_op jit(solution)/shard_map/pallas_call | solution.py:188
  1.6 32.7 %all_to_all.15 = bf16[128,8,128]{2,1,0:T(8,128)(2,1)S(1)} all-to-all(bf16[128,8,128]{2,1,0:T(8,128)(2,1)S(1)} %bitcast.18), channel_id=1, replica_groups=mesh['yh'=2,'z2'=2,'z1'=2,'z0'=2,'y1'=2,'y0'=2,'x1'=2,'x0'=2,'co'=2] {'y..., dimensions={0} | all-to-all | bytes 524288 | tf_op jit(solution)/shard_map/all_to_all | solution.py:230
  34.3 0.7 %shard_map.92 = bf16[512,512]{1,0:T(8,128)(2,1)S(1)} custom-call(bf16[1024,128]{1,0:T(8,128)(2,1)S(1)} %bitcast.15), custom_call_target="tpu_custom_call" | custom-call | flops 1000000 | bytes 1048576 | tf_op jit(solution)/shard_map/pallas_call | solution.py:188
  35.0 13.6 %all_to_all.16 = bf16[8,64,512]{2,1,0:T(8,128)(2,1)S(1)} all-to-all(bf16[8,64,512]{2,1,0:T(8,128)(2,1)S(1)} %bitcast.14), channel_id=1, replica_groups=mesh['yh'=2,'z2'=2,'z1'=2,'z0'=2,'y1'=2,'y0'=2,'x1'=2,'x0'=2,'co'=2] {'x..., dimensions={0} | all-to-all | bytes 1048576 | tf_op jit(solution)/shard_map/all_to_all | solution.py:235
  48.6 0.3 shard_map.93
  49.0 0.0 copy-start
  49.0 0.0 copy-start.1
  49.0 15.6 %all_to_all.17 = bf16[64,8,128]{2,1,0:T(8,128)(2,1)S(1)} all-to-all(bf16[64,8,128]{2,1,0:T(8,128)(2,1)S(1)} %bitcast.17), channel_id=1, replica_groups=mesh['yh'=2,'z2'=2,'z1'=2,'z0'=2,'y1'=2,'y0'=2,'x1'=2,'x0'=2,'co'=2] {'y..., dimensions={0} | all-to-all | bytes 262144 | tf_op jit(solution)/shard_map/all_to_all | solution.py:241
  64.6 0.0 copy-done
  64.6 0.0 copy-done.1
  64.6 1.1 %shard_map.94 = bf16[512,128]{1,0:T(8,128)(2,1)} custom-call(bf16[512,128]{1,0:T(8,128)(2,1)S(1)} %bitcast.16, bf16[512,128]{1,0:T(8,128)(2,1)S(1)} %get-tuple-element.9.normed, bf16[128,128]{1,0:T(8,128)(2,1)S(1)} %copy-done, f32[2,128]{1,0:T(2,128)S(1)} %get-tuple-element.10.scales, bf16[128,128]{1,0:T(8,128)(2,1)S(1)} %copy-done.1), custom_call_target="tpu_custom_call" | custom-call | flops 1000000 | bytes 1048576 | tf_op jit(solution)/shard_map/pallas_call | solution.py:188
Async XLA Ops:
  49.0 15.7 %copy-start = (bf16[128,128]{1,0:T(8,128)(2,1)S(1)}, bf16[128,128]{1,0:T(8,128)(2,1)}, u32[]{:S(2)}) copy-start(bf16[128,128]{1,0:T(8,128)(2,1)} %gate_weight.1) | copy-start | bytes 98308
  49.0 15.6 %copy-start.1 = (bf16[128,128]{1,0:T(8,128)(2,1)S(1)}, bf16[128,128]{1,0:T(8,128)(2,1)}, u32[]{:S(2)}) copy-start(bf16[128,128]{1,0:T(8,128)(2,1)} %out_weight.1) | copy-start | bytes 98308
